TPU v7x, 32 devices: a whole 2x2x4 slice. The times are simulated.
32 devices in a mesh: dp: 4 (over x, core), rows: 8 (over z, y).
Axes of the slice: x: 2, y: 2, z: 4, core: 2. Of those that a mesh axis runs over, the one named last changes fastest.
Arguments:
- item_table: float32 [131072, 128], P(('dp', 'rows')), may hold values from -3 to 3
- adagrad_state: float32 [131072, 128], P(('dp', 'rows')), may hold values from 0.0001 to 0.01
- history_ids: int32 [4096, 50], P(('dp', 'rows')), may hold values from 0 to 131071, as said below
- positive_ids: int32 [4096], P(('dp', 'rows')), may hold values from 0 to 131071, as said below
Outputs:
- new_table: float32 [131072, 128], P(('dp', 'rows'))
- new_state: float32 [131072, 128], P(('dp', 'rows'))
Inputs may be any that keep to these rules, and one draw needn't show every extreme that they name: `history_ids`: ids are counted over one device's 128 users (an aligned block of users), history and positive together, with repeats. In every such block, at most 512 ids have any one value of id // 4096, and some value has exactly 512; one value has exactly 512 in every block. Popular items repeat. `positive_ids`: counted together with history_ids as stated there.
All inputs are finite; a program needn't handle non-finite values.
Results may differ from a plain program's by a relative error of at most 0.00012.
Values sent between devices are 32-bit elements; how exact they have to be, the bound alone decides.
A program may use at most 128 MiB of HBM per device.

v0:
```python
import functools

import jax
import jax.numpy as jnp
from jax import lax
from jax.experimental import pallas as pl
from jax.experimental.pallas import tpu as pltpu
from jax.sharding import PartitionSpec as P

penalty_weight = 10.0
step_size = 0.05
LOW = 128
STREAMS = 8
HIGHEST = lax.Precision.HIGHEST
f32, bf16, i32 = jnp.float32, jnp.bfloat16, jnp.int32


def round_up(value, unit):
    return (value + unit - 1) // unit * unit


def route_kernel(devices, capacity, users_dev, block, owner_ref, local_ref, code_ref, out_ref, acc):
    blocks = owner_ref.shape[1] // block
    upper = (
        lax.broadcasted_iota(i32, (block, block), 0) <= lax.broadcasted_iota(i32, (block, block), 1)
    ).astype(bf16)
    owners = lax.broadcasted_iota(i32, (devices, block), 0)
    ranks_to = lax.broadcasted_iota(i32, (capacity, block), 0)
    acc[...] = jnp.zeros_like(acc)
    carry = jnp.zeros((devices, 1), f32)
    for j in range(blocks):
        cols = slice(j * block, (j + 1) * block)
        local = local_ref[:, cols]
        high = (local // LOW).astype(f32)
        low = (local % LOW).astype(f32)
        code = code_ref[:, cols].astype(f32)
        member = (owner_ref[:, cols] == owners).astype(f32)
        prefix = jnp.dot(member.astype(bf16), upper, preferred_element_type=f32)
        rank = jnp.sum(member * (prefix + carry), axis=0, keepdims=True) - 1.0
        carry = carry + jnp.sum(member, axis=1, keepdims=True)
        left = jnp.concatenate(
            [member * high, member * low, member * code, member], axis=0
        ).astype(bf16)
        right = (rank.astype(i32) == ranks_to).astype(f32).astype(bf16)
        acc[...] += lax.dot_general(
            left, right, (((1,), (1,)), ((), ())), preferred_element_type=f32
        )
    row = acc[0:devices] * LOW + acc[devices : 2 * devices]
    code = acc[2 * devices : 3 * devices]
    present = acc[3 * devices : 4 * devices]
    empty = 2 * users_dev
    out_ref[0] = row.astype(i32)
    out_ref[1] = jnp.where(present > 0.5, code, float(empty)).astype(i32)


def split2(x):
    hi = x.astype(bf16)
    return hi, (x - hi.astype(f32)).astype(bf16)


def partial_kernel(devices, capacity, groups, unroll, rows_ref, code_ref, gram_ref, table_ref, out_ref, picked):
    width = table_ref.shape[1]
    codes_to = lax.broadcasted_iota(i32, (groups, capacity), 0)

    def one(b, _):
        base = b * capacity

        def gather(s, _):
            for k in range(unroll):
                e = s * unroll + k
                r = rows_ref[base + e]
                picked[pl.ds(e, 1), :] = table_ref[pl.ds(r, 1), :]
            return 0

        lax.fori_loop(0, capacity // unroll, gather, 0)
        x = picked[...]
        a0, a1 = split2(x)
        a2 = (x - a0.astype(f32) - a1.astype(f32)).astype(bf16)
        hot = (code_ref[b] == codes_to).astype(f32).astype(bf16)
        both = jnp.dot(hot, jnp.concatenate([a0, a1], axis=1), preferred_element_type=f32)
        last = jnp.dot(hot, a2, preferred_element_type=f32)
        out_ref[b, 0:groups, :] = both[:, :width] + (both[:, width:] + last)
        out_ref[b, groups:, :] = gram_ref[b]
        return 0

    lax.fori_loop(0, devices, one, 0)


def reduce_kernel(data, shard, part_ref, out_ref, held, got, send1, recv1, send2, recv2, send3, recv3, send4, recv4):
    peers = data // 2 * shard
    dp, rw = lax.axis_index("dp"), lax.axis_index("rows")
    core = lax.rem(dp, 2)
    flat = dp // 2 * shard + rw
    other = (dp + 1 - 2 * core, rw)
    mesh_id = pl.DeviceIdType.MESH

    def place(k):
        at = lax.rem(flat + k, peers)
        return at // shard * 2 + core, lax.rem(at, shard)

    def slab(k, side):
        d, r = place(k)
        return (d + (1 - 2 * core) * side) * shard + r

    barrier = pltpu.get_barrier_semaphore()
    pl.semaphore_signal(barrier, inc=1, device_id=other, device_id_type=mesh_id)

    def greet(k, _):
        pl.semaphore_signal(barrier, inc=1, device_id=place(k), device_id_type=mesh_id)
        return 0

    lax.fori_loop(1, peers, greet, 0)
    pl.semaphore_wait(barrier, peers)

    def remote(src, dst, send, recv, device):
        return pltpu.make_async_remote_copy(
            src_ref=src, dst_ref=dst, send_sem=send, recv_sem=recv, device_id=device, device_id_type=mesh_id
        )

    def copy1(k):
        return remote(part_ref.at[slab(k, 1)], held.at[k], send1.at[k], recv1.at[k], other)

    def copy2(k):
        return remote(held.at[k], got.at[k], send2.at[k], recv2.at[k], place(k))

    def copy3(k):
        mine = out_ref.at[slab(0, 0)]
        return remote(mine, mine, send3.at[k], recv3.at[k], place(k))

    def copy4(k):
        at = out_ref.at[slab(peers - k, 0)]
        return remote(at, at, send4.at[k], recv4.at[k], other)

    def each(first, count, act):
        def step(k, _):
            act(k)
            return 0

        lax.fori_loop(first, count, step, 0)

    def start1(k):
        copy1(lax.rem(k, peers)).start()

    each(1, peers + 1, start1)

    def pair(k):
        copy1(k).wait_recv()
        held[k] = held[k] + part_ref[slab(k, 0)]
        copy2(k).start()

    each(1, peers, pair)
    copy1(0).wait_recv()
    held[0] = held[0] + part_ref[slab(0, 0)]

    def gain(k):
        copy2(k).wait_recv()
        held[0] = held[0] + got[k]

    each(1, peers, gain)
    out_ref[slab(0, 0)] = held[0]
    each(1, peers, lambda k: copy3(k).start())
    copy4(0).start()

    def forward(k):
        copy3(k).wait_recv()
        copy4(k).start()

    each(1, peers, forward)
    each(0, peers, lambda k: copy4(k).wait_recv())

    def drain(k):
        copy1(k).wait_send()
        copy4(k).wait_send()

    each(0, peers, drain)

    def drain2(k):
        copy2(k).wait_send()
        copy3(k).wait_send()

    each(1, peers, drain2)


def update_kernel(
    devices, users_dev, hist_len, coef, entries, unroll,
    rows_ref, gidx_ref, sums_ref, table_ref, state_ref, new_table_ref, new_state_ref,
    grads, ugram, *accs,
):
    groups = 2 * users_dev
    total = devices * groups
    extra = sums_ref.shape[1] - groups
    for t in range(ugram.shape[0] // extra):
        ugram[t * extra : (t + 1) * extra, :] = sums_ref[t, groups:, :]
    item_total = ugram[...]
    ugram[...] = jnp.zeros_like(ugram)
    grads[pl.ds(total, 8), :] = jnp.zeros((8, grads.shape[1]), f32)

    def user(b, _):
        at = pl.multiple_of(b * groups, 8)
        at2 = pl.multiple_of(b * groups + users_dev, 8)
        uv = sums_ref[b, 0:users_dev, :] / hist_len
        pv = sums_ref[b, users_dev:groups, :]
        gap = jnp.sum(uv * pv, axis=1, keepdims=True) - 1.0
        ug = 2.0 * gap * pv + 2.0 * coef * jnp.dot(
            uv, item_total, precision=HIGHEST, preferred_element_type=f32
        )
        grads[pl.ds(at, users_dev), :] = ug / hist_len
        grads[pl.ds(at2, users_dev), :] = 2.0 * gap * uv
        ugram[...] += lax.dot_general(
            uv, uv, (((0,), (0,)), ((), ())), precision=HIGHEST, preferred_element_type=f32
        )
        return 0

    lax.fori_loop(0, devices, user, 0)
    for acc in accs:
        acc[...] = jnp.zeros_like(acc)
    part = entries // len(accs)

    def scatter(s, _):
        for q in range(unroll):
            rows = [rows_ref[k * part + s * unroll + q] for k in range(len(accs))]
            gidx = [gidx_ref[k * part + s * unroll + q] for k in range(len(accs))]
            vals = [
                acc[pl.ds(r, 1), :] + grads[pl.ds(g, 1), :] for acc, r, g in zip(accs, rows, gidx)
            ]
            for acc, r, v in zip(accs, rows, vals):
                acc[pl.ds(r, 1), :] = v
        return 0

    lax.fori_loop(0, part // unroll, scatter, 0)
    tile = 256
    rows_dev = table_ref.shape[0]
    user_total = ugram[...]

    def finish(t, _):
        at = pl.ds(pl.multiple_of(t * tile, 8), tile)
        item = table_ref[at, :]
        g = 2.0 * coef * jnp.dot(item, user_total, precision=HIGHEST, preferred_element_type=f32)
        add = accs[0][at, :]
        for acc in accs[1:]:
            add = add + acc[at, :]
        g = g + add
        state = state_ref[at, :] + g * g
        new_state_ref[at, :] = state
        new_table_ref[at, :] = item - step_size * g / jnp.sqrt(state)
        return 0

    lax.fori_loop(0, rows_dev // tile, finish, 0)


VM = pl.BlockSpec(memory_space=pltpu.VMEM)
SM = pl.BlockSpec(memory_space=pltpu.SMEM)
PARAMS = pltpu.CompilerParams(vmem_limit_bytes=60 * 1024 * 1024)


def shards(item_table, adagrad_state, history_ids, positive_ids):
    rows_dev, width = item_table.shape
    users_dev, hist_len = history_ids.shape
    devices = lax.axis_size("dp") * lax.axis_size("rows")
    groups = 2 * users_dev
    count = users_dev * (hist_len + 1)
    capacity = max(8, (count * 5 // (2 * devices) + 7) // 8 * 8)
    block = 512
    padded = round_up(count, block)
    requests = jnp.concatenate([history_ids.reshape(-1), positive_ids])
    code = jnp.concatenate(
        [jnp.arange(users_dev * hist_len, dtype=i32) // hist_len, users_dev + jnp.arange(users_dev, dtype=i32)]
    )
    requests = jnp.pad(requests, (0, padded - count), constant_values=devices * rows_dev)
    code = jnp.pad(code, (0, padded - count))
    owner = requests // rows_dev
    local = requests - owner * rows_dev

    lists = pl.pallas_call(
        functools.partial(route_kernel, devices, capacity, users_dev, block),
        out_shape=jax.ShapeDtypeStruct((2, devices, capacity), i32),
        in_specs=[VM] * 3,
        out_specs=VM,
        scratch_shapes=[pltpu.VMEM((4 * devices, capacity), f32)],
        compiler_params=PARAMS,
        name="route",
    )(owner[None], local[None], code[None])
    asked = lax.all_to_all(lists, ("dp", "rows"), split_axis=1, concat_axis=1, tiled=True)
    rows = asked[0].reshape(-1)
    codes = asked[1]
    entries = devices * capacity
    item_gram = jnp.dot(item_table.T, item_table, precision=HIGHEST, preferred_element_type=f32)
    extra = round_up(-(-width // devices), 8)
    chunk = groups + extra
    gram_rows = jnp.pad(item_gram, ((0, devices * extra - width), (0, 0))).reshape(devices, extra, width)
    partial = pl.pallas_call(
        functools.partial(partial_kernel, devices, capacity, groups, 32),
        out_shape=jax.ShapeDtypeStruct((devices, chunk, width), f32),
        in_specs=[SM, VM, VM, VM],
        out_specs=VM,
        scratch_shapes=[pltpu.VMEM((capacity, width), f32)],
        compiler_params=PARAMS,
        name="partial",
    )(rows, codes[:, None, :], gram_rows, item_table)
    data, shard = lax.axis_size("dp"), lax.axis_size("rows")
    peers = devices // 2
    sums = pl.pallas_call(
        functools.partial(reduce_kernel, data, shard),
        out_shape=jax.ShapeDtypeStruct((devices, chunk, width), f32),
        in_specs=[VM],
        out_specs=VM,
        scratch_shapes=[pltpu.VMEM((peers, chunk, width), f32)] * 2 + [pltpu.SemaphoreType.DMA((peers,))] * 8,
        compiler_params=pltpu.CompilerParams(
            vmem_limit_bytes=60 * 1024 * 1024, collective_id=0, has_side_effects=True
        ),
        name="reduce",
    )(partial)
    coef = penalty_weight / (rows_dev * devices)
    gidx = jnp.where(
        codes < groups, codes + groups * jnp.arange(devices, dtype=i32)[:, None], devices * groups
    ).reshape(-1)
    return pl.pallas_call(
        functools.partial(update_kernel, devices, users_dev, hist_len, coef, entries, 4),
        out_shape=(
            jax.ShapeDtypeStruct(item_table.shape, f32),
            jax.ShapeDtypeStruct(item_table.shape, f32),
        ),
        in_specs=[SM, SM, VM, VM, VM],
        out_specs=(VM, VM),
        scratch_shapes=[
            pltpu.VMEM((devices * groups + 8, width), f32),
            pltpu.VMEM((width, width), f32),
        ]
        + [pltpu.VMEM((rows_dev, width), f32)] * STREAMS,
        compiler_params=PARAMS,
        name="update",
    )(rows, gidx, sums, item_table, adagrad_state)


def solution(mesh):
    return jax.shard_map(
        shards,
        mesh=mesh,
        in_specs=(
            P(("dp", "rows"), None),
            P(("dp", "rows"), None),
            P(("dp", "rows"), None),
            P(("dp", "rows")),
        ),
        out_specs=(P(("dp", "rows"), None), P(("dp", "rows"), None)),
        check_vma=False,
    )
```

profile of v0, /device:TPU:29, one launch (start us, length us, event | category | flops | bytes accessed | tf_op | source)
XLA Modules:
  0.0 217.0 jit_solution(5536981369876161290)
XLA Ops:
  0.7 0.6 broadcast_in_dim.16.code_ref
  1.3 0.8 copy.7
  2.2 0.1 reshape.18
  2.3 0.7 pad_add_fusion
  3.0 0.6 broadcast_in_dim.15.local_ref
  3.6 0.6 broadcast_in_dim.14.owner_ref
  4.2 6.1 %route.1 = s32[2,32,512]{2,1,0:T(8,128)} custom-call(s32[1,6656]{1,0:T(1,128)} %broadcast_in_dim.14.owner_ref, s32[1,6656]{1,0:T(1,128)} %broadcast_in_dim.15.local_ref, s32[1,6656]{1,0:T(1,128)} %broadcast_in_dim.16.code_ref), custom_call_target="tpu_custom_call" | custom-call | tf_op jit(solution)/shard_map/route/pallas_call | solution.py:274
  10.4 1.7 copy.8
  12.0 6.1 %all-to-all-start = ((s32[2,32,512]{2,0,1:T(2,128)}), s32[2,32,512]{2,0,1:T(2,128)S(1)}, u32[]{:S(2)}, u32[]{:S(2)}) async-start(s32[2,32,512]{2,0,1:T(2,128)} %copy.8), calls=%async_computation | async-start | bytes 262144 | tf_op jit(solution)/shard_map/all_to_all | solution.py:283
  18.2 5.7 %fusion.5 = f32[128,128]{1,0:T(8,128)S(1)} fusion(f32[4096,128]{1,0:T(8,128)} %table_ref.3), kind=kOutput, calls=%fused_computation.23 | convolution fusion | flops 805306368 | bytes 2162688 | tf_op jit(solution)/shard_map/dot_general | solution.py:287
  23.9 0.1 broadcast_bitcast_fusion
  24.0 0.7 pad_bitcast_fusion.gram_ref
  24.6 0.0 all-to-all-done
  24.6 0.8 slice_bitcast_fusion
  25.4 33.3 %partial.1.part_ref = f32[32,264,128]{2,1,0:T(8,128)} custom-call(s32[16384]{0:T(1024)} %bitcast.11, s32[32,1,512]{2,1,0:T(1,128)} %get-tuple-element.2.code_ref, f32[32,8,128]{2,1,0:T(8,128)} %pad_bitcast_fusion.gram_ref, f32[4096,128]{1,0:T(8,128)} %table_ref.3), custom_call_target="tpu_custom_call" | custom-call | tf_op jit(solution)/shard_map/partial/pallas_call | solution.py:291
  58.7 111.7 %reduce.1.sums_ref = f32[32,264,128]{2,1,0:T(8,128)} custom-call(f32[32,264,128]{2,1,0:T(8,128)} %partial.1.part_ref), custom_call_target="tpu_custom_call" | custom-call | tf_op jit(solution)/shard_map/reduce/pallas_call | solution.py:302
  170.3 0.6 add_select_fusion.gidx_ref
  171.0 46.0 %update.1 = (f32[4096,128]{1,0:T(8,128)}, f32[4096,128]{1,0:T(8,128)}) custom-call(s32[16384]{0:T(1024)} %bitcast.12, s32[16384]{0:T(1024)} %add_select_fusion.gidx_ref, f32[32,264,128]{2,1,0:T(8,128)} %reduce.1.sums_ref, f32[4096,128]{1,0:T(8,128)} %table_ref.3, f32[4096,128]{1,0:T(8,128)} %state_ref.1), custom_call_target="tpu_custom_call" | custom-call | tf_op jit(solution)/shard_map/update/pallas_call | solution.py:317
  (7 shorter events, 0.1 us)
Async XLA Ops:
  12.0 12.6 %all-to-all-start = ((s32[2,32,512]{2,0,1:T(2,128)}), s32[2,32,512]{2,0,1:T(2,128)S(1)}, u32[]{:S(2)}, u32[]{:S(2)}) async-start(s32[2,32,512]{2,0,1:T(2,128)} %copy.8), calls=%async_computation | async-start | bytes 262144 | tf_op jit(solution)/shard_map/all_to_all | solution.py:283
where the time goes:
time: 217 us
  Pallas kernels  197 us (91%)
  starting transfers between devices  6.13 us (3%)
  local copies, waits for them, and re-layouts  6.04 us (3%)
  matrix products  5.67 us (3%)
    pallas_call x1, Pallas kernels, shards(): pl.pallas_call(functools.partial(reduce_kernel, data, shard), out_shape=j...  112 us
    pallas_call x1, Pallas kernels, shards(): pl.pallas_call(functools.partial(update_kernel, devices, users_dev, hist_...  46 us
    pallas_call x1, Pallas kernels, shards(): pl.pallas_call(functools.partial(partial_kernel, devices, capacity, group...  33.3 us
    pallas_call x1, Pallas kernels, shards(): pl.pallas_call(functools.partial(route_kernel, devices, capacity, users_d...  6.14 us
    all_to_all x1, starting transfers between devices, shards(): lax.all_to_all(lists, ('dp', 'rows'), split_axis=1, concat_axis=1, tiled=...  6.13 us
    dot_general x1, matrix products, shards(): jnp.dot(item_table.T, item_table, precision=HIGHEST, preferred_element_ty...  5.67 us
  transfers between devices with their start and end apart: 1, of which 0 were waited for; matrix products, arithmetic and copies ran while one was open for 3% of the time, Pallas kernels for 0%

commit v1 on v0

v1 whole, which is shorter than its diff:
```python
import functools

import jax
import jax.numpy as jnp
from jax import lax
from jax.experimental import pallas as pl
from jax.experimental.pallas import tpu as pltpu
from jax.sharding import PartitionSpec as P

penalty_weight = 10.0
step_size = 0.05
LOW = 128
STREAMS = 8
HIGHEST = lax.Precision.HIGHEST
f32, bf16, i32 = jnp.float32, jnp.bfloat16, jnp.int32


def round_up(value, unit):
    return (value + unit - 1) // unit * unit


def route_kernel(devices, capacity, users_dev, block, owner_ref, local_ref, code_ref, out_ref, acc):
    blocks = owner_ref.shape[1] // block
    upper = (
        lax.broadcasted_iota(i32, (block, block), 0) <= lax.broadcasted_iota(i32, (block, block), 1)
    ).astype(bf16)
    owners = lax.broadcasted_iota(i32, (devices, block), 0)
    ranks_to = lax.broadcasted_iota(i32, (capacity, block), 0)
    acc[...] = jnp.zeros_like(acc)
    carry = jnp.zeros((devices, 1), f32)
    for j in range(blocks):
        cols = slice(j * block, (j + 1) * block)
        local = local_ref[:, cols]
        high = (local // LOW).astype(f32)
        low = (local % LOW).astype(f32)
        code = code_ref[:, cols].astype(f32)
        member = (owner_ref[:, cols] == owners).astype(f32)
        prefix = jnp.dot(member.astype(bf16), upper, preferred_element_type=f32)
        rank = jnp.sum(member * (prefix + carry), axis=0, keepdims=True) - 1.0
        carry = carry + jnp.sum(member, axis=1, keepdims=True)
        left = jnp.concatenate(
            [member * high, member * low, member * code, member], axis=0
        ).astype(bf16)
        right = (rank.astype(i32) == ranks_to).astype(f32).astype(bf16)
        acc[...] += lax.dot_general(
            left, right, (((1,), (1,)), ((), ())), preferred_element_type=f32
        )
    row = acc[0:devices] * LOW + acc[devices : 2 * devices]
    code = acc[2 * devices : 3 * devices]
    present = acc[3 * devices : 4 * devices]
    empty = 2 * users_dev
    out_ref[0] = row.astype(i32)
    out_ref[1] = jnp.where(present > 0.5, code, float(empty)).astype(i32)


def split2(x):
    hi = x.astype(bf16)
    return hi, (x - hi.astype(f32)).astype(bf16)


def line_sizes(data, shard):
    cols = max(n for n in range(1, shard + 1) if shard % n == 0 and n * n <= shard)
    return data // 2, cols, shard // cols


ORDERS = ((0, 1, 2), (1, 2, 0))
LAGS = (2, 4, 6, 8)
VSLOTS = 4


def exchange_kernel(
    sizes, capacity, users_dev, hist_len, coef, unroll,
    rows_ref, codes_ref, hot_ref, gram_ref, table_ref, vals_ref, ugram_ref,
    picked, part, pair, mail, grads, cur, vbuf, upart, gsum, gmail, gfull,
    pair_send, pair_recv, mail_send, mail_recv, ag_send, ag_recv, twin_send, twin_recv, gram_send, gram_recv, vsem,
):
    nx, ny, nz = sizes
    plane = nx * ny * nz
    shard = ny * nz
    width = table_ref.shape[1]
    half = width // 2
    dp, rw = lax.axis_index("dp"), lax.axis_index("rows")
    core = lax.rem(dp, 2)
    pos = (dp // 2, lax.rem(rw, ny), rw // ny)
    origin = (0, 0, 0)
    axes = (0, 1, 2)

    def device(chip, c):
        return chip[0] * 2 + c, chip[2] * ny + chip[1]

    def block(chip, c):
        d, r = device(chip, c)
        return d * shard + r

    def ahead(r):
        return tuple(lax.rem(p + k, n) for p, k, n in zip(pos, r, sizes))

    def behind(o):
        return tuple(lax.rem(p - k + n, n) for p, k, n in zip(pos, o, sizes))

    def only(a, k):
        return tuple(k if b == a else 0 for b in axes)

    def add(r, a, k):
        return tuple(v + k if b == a else v for b, v in enumerate(r))

    def slot(r):
        return (r[0] * ny + r[1]) * nz + r[2]

    def unslot(at):
        return at // (ny * nz), lax.rem(at // nz, ny), lax.rem(at, nz)

    partner = device(pos, 1 - core)

    def remote(src, dst, send, recv, dev):
        return pltpu.make_async_remote_copy(
            src_ref=src, dst_ref=dst, send_sem=send, recv_sem=recv,
            device_id=dev, device_id_type=pl.DeviceIdType.MESH,
        )

    def each(first, count, act):
        def step(k, _):
            act(k)
            return 0

        lax.fori_loop(first, count, step, 0)

    barrier = pltpu.get_barrier_semaphore()
    greeted = 1
    pl.semaphore_signal(barrier, inc=1, device_id=partner, device_id_type=pl.DeviceIdType.MESH)
    for a in axes:
        for k in range(1, sizes[a]):
            greeted += 1
            pl.semaphore_signal(
                barrier, inc=1, device_id=device(ahead(only(a, k)), core), device_id_type=pl.DeviceIdType.MESH
            )
    pl.semaphore_wait(barrier, greeted)

    def pair_copy(at):
        return remote(part.at[0, at], pair.at[at], pair_send.at[at], pair_recv.at[at], partner)

    def letter(h, at, dev):
        return remote(part.at[1, at, h], mail.at[h, at], mail_send.at[h, at], mail_recv.at[h, at], dev)

    def parcel(h, at, b, dev):
        return remote(grads.at[b, h], grads.at[b, h], ag_send.at[h, at], ag_recv.at[h, at], dev)

    def twin(at, b):
        return remote(grads.at[b], grads.at[b], twin_send.at[at], twin_recv.at[at], partner)

    first = [1]
    for a in axes:
        first.append(first[-1] + sizes[a] - 1)
    last = first[3]
    mine = pl.ds(pl.multiple_of(core * half, 8), half)
    theirs = pl.ds(pl.multiple_of((1 - core) * half, 8), half)

    def gram_pair(t, src):
        return remote(src.at[theirs], gmail.at[t, 0], gram_send.at[t, 0], gram_recv.at[t, 0], partner)

    def gram_line(t, a, k):
        at = first[a] + k - 1
        return remote(
            gsum.at[t, a], gmail.at[t, at], gram_send.at[t, at], gram_recv.at[t, at], device(ahead(only(a, k)), core)
        )

    def gram_final(t):
        return remote(gsum.at[t, 3], gfull.at[t, mine], gram_send.at[t, last], gram_recv.at[t, last], partner)

    def gram_open(t, src):
        gram_pair(t, src).start()

    def gram_send_line(t, a):
        for k in range(1, sizes[a]):
            gram_line(t, a, k).start()

    def gram_step(t, src, stage):
        if stage == 0:
            gram_pair(t, src).wait_recv()
            gsum[t, 0] = src[mine, :] + gmail[t, 0]
        elif stage <= 3:
            a = stage - 1
            total = gsum[t, a]
            for k in range(1, sizes[a]):
                gram_line(t, a, k).wait_recv()
                total = total + gmail[t, first[a] + k - 1]
            gsum[t, a + 1] = total
        else:
            gram_final(t).wait_recv()
        if stage < 3:
            gram_send_line(t, stage)
        elif stage == 3:
            gram_final(t).start()
            gfull[t, mine] = gsum[t, 3]

    def gram_drain(t, src):
        gram_pair(t, src).wait_send()
        for a in axes:
            for k in range(1, sizes[a]):
                gram_line(t, a, k).wait_send()
        gram_final(t).wait_send()

    codes_to = lax.broadcasted_iota(i32, (2 * users_dev, capacity), 0)

    def gather(b, j, at):
        base = b * capacity

        def some(s, _):
            start = base + s * unroll
            for k in range(unroll):
                r = rows_ref[start + k]
                picked[pl.ds(s * unroll + k, 1), :] = table_ref[pl.ds(r, 1), :]
            return 0

        lax.fori_loop(0, capacity // unroll, some, 0)
        x = picked[...]
        hi, lo = split2(x)
        hot = (hot_ref[b] == codes_to).astype(f32).astype(bf16)
        both = jnp.dot(hot, jnp.concatenate([hi, lo], axis=1), preferred_element_type=f32)
        out = both[:, :width] + both[:, width:]
        part[j, at, 0] = out[:users_dev]
        part[j, at, 1] = out[users_dev:]

    def arrive(h, r, a):
        at = slot(r)
        for k in range(1, sizes[a]):
            m = slot(add(r, a, k))
            letter(h, m, partner).wait_recv()
            part[1, at, h] = part[1, at, h] + mail[h, m]

    def leave(h, r, a):
        @pl.when(r[a] != 0)
        def _():
            chip = tuple(lax.rem(p + r[a], n) if b == a else p for b, (p, n) in enumerate(zip(pos, sizes)))
            letter(h, slot(r), device(chip, core)).start()

    gram_open(0, gram_ref)

    def reduce_step(i, _):
        for stage in range(4):
            j = i - LAGS[stage]
            at = plane - 1 - j

            @pl.when(jnp.logical_and(j >= 0, j < plane))
            def _():
                r = unslot(at)
                if stage == 0:
                    pair_copy(at).wait_recv()
                    for h in range(2):
                        part[1, at, h] = part[1, at, h] + pair[at, h]
                        leave(h, r, ORDERS[h][0])
                else:
                    for h in range(2):
                        order = ORDERS[h]
                        clear = r[order[0]] == 0
                        for a in order[1:stage]:
                            clear = jnp.logical_and(clear, r[a] == 0)

                        @pl.when(clear)
                        def _():
                            arrive(h, r, order[stage - 1])
                            if stage < 3:
                                leave(h, r, order[stage])

        for stage in range(5):
            @pl.when(i == 2 * stage + 2)
            def _():
                gram_step(0, gram_ref, stage)

        @pl.when(i < plane)
        def _():
            at = plane - 1 - i
            chip = ahead(unslot(at))

            def one(j, _):
                c = (1 - core) * (1 - j) + core * j
                gather(block(chip, c), j, at)

                @pl.when(j == 0)
                def _():
                    pair_copy(at).start()

                return 0

            lax.fori_loop(0, 2, one, 0)

        return 0

    lax.fori_loop(0, plane + LAGS[3], reduce_step, 0)

    me = block(pos, core)
    uv = part[1, 0, 0] / hist_len
    pv = part[1, 0, 1]
    gap = jnp.sum(uv * pv, axis=1, keepdims=True) - 1.0
    ug = 2.0 * gap * pv + 2.0 * coef * jnp.dot(uv, gfull[0], precision=HIGHEST, preferred_element_type=f32)
    grads[me, 0] = ug / hist_len
    grads[me, 1] = 2.0 * gap * uv

    def forward(h, o, b, a):
        for k in range(1, sizes[a]):
            chip = tuple(lax.rem(p + k, n) if c == a else p for c, (p, n) in enumerate(zip(pos, sizes)))
            parcel(h, slot(add(o, a, k)), b, device(chip, core)).start()

    def received(h, o):
        b = block(behind(o), core)
        parcel(h, slot(o), b, partner).wait_recv()
        return b

    ways = tuple(order[::-1] for order in ORDERS)
    for a in range(3):
        for h in range(2):
            forward(h, origin, me, ways[h][a])
    twin(0, me).start()
    upart[...] = lax.dot_general(
        uv, uv, (((0,), (0,)), ((), ())), precision=HIGHEST, preferred_element_type=f32
    )
    gram_open(1, upart)
    cur[pl.ds(2 * users_dev, 8), :] = jnp.zeros((8, width), f32)

    def vals_copy(v, b):
        return pltpu.make_async_copy(vbuf.at[v], vals_ref.at[b], vsem.at[v])

    def vals(n, b):
        v = lax.rem(n, VSLOTS)

        @pl.when(n >= VSLOTS)
        def _():
            vals_copy(v, b).wait()

        cur[pl.ds(0, users_dev), :] = grads[b, 0]
        cur[pl.ds(users_dev, users_dev), :] = grads[b, 1]
        base = b * capacity

        def some(s, _):
            start = base + s * unroll
            for k in range(unroll):
                c = codes_ref[start + k]
                vbuf[v, pl.ds(s * unroll + k, 1), :] = cur[pl.ds(c, 1), :]
            return 0

        lax.fori_loop(0, capacity // unroll, some, 0)
        vals_copy(v, b).start()

    for h in range(2):
        a1, a2, a3 = ways[h]
        for k in range(1, sizes[a1]):
            o = only(a1, k)
            b = received(h, o)
            forward(h, o, b, a2)
            forward(h, o, b, a3)
    gram_step(1, upart, 0)
    for h in range(2):
        a1, a2, a3 = ways[h]
        for k in range(1, sizes[a2]):
            for m in range(sizes[a1]):
                o = add(only(a2, k), a1, m)
                b = received(h, o)
                forward(h, o, b, a3)
        gram_step(1, upart, h + 1)

    def spread(n, _):
        @pl.when(n < plane)
        def _():
            o = unslot(n)
            b = block(behind(o), core)
            for h in range(2):
                @pl.when(o[ways[h][2]] != 0)
                def _():
                    received(h, o)

            @pl.when(n > 0)
            def _():
                twin(n, b).start()

            vals(2 * n, b)

        @pl.when(n > 0)
        def _():
            o = unslot(n - 1)
            b = block(behind(o), 1 - core)
            twin(n - 1, b).wait_recv()
            vals(2 * n - 1, b)

        for stage in (3, 4):
            @pl.when(n == 4 * (stage - 2))
            def _():
                gram_step(1, upart, stage)

        return 0

    lax.fori_loop(0, plane + 1, spread, 0)
    ugram_ref[...] = gfull[1]

    def drain(n):
        pair_copy(n).wait_send()
        twin(n, me).wait_send()

    each(0, plane, drain)

    def drain_mail(n):
        for h in range(2):
            letter(h, n, partner).wait_send()
            parcel(h, n, me, partner).wait_send()

    each(1, plane, drain_mail)
    gram_drain(0, gram_ref)
    gram_drain(1, upart)
    each(0, VSLOTS, lambda v: vals_copy(v, me).wait())


def scatter_kernel(
    coef, chunk, unroll, tile,
    rows_ref, vals_ref, ugram_ref, table_ref, state_ref, new_table_ref, new_state_ref,
    vbuf, table, state, vsem, in_sem, out_sem, *accs,
):
    entries = rows_ref.shape[0]
    chunks = entries // chunk
    part = chunk // len(accs)
    rows_dev, width = table.shape
    tiles = rows_dev // tile

    def vals_copy(n):
        s = lax.rem(n, 2)
        return pltpu.make_async_copy(
            vals_ref.at[pl.ds(pl.multiple_of(n * chunk, 8), chunk)], vbuf.at[s], vsem.at[s]
        )

    table_copy = pltpu.make_async_copy(table_ref, table, in_sem.at[0])
    state_copy = pltpu.make_async_copy(state_ref, state, in_sem.at[1])
    vals_copy(0).start()
    vals_copy(1).start()
    table_copy.start()
    state_copy.start()
    for acc in accs:
        acc[...] = jnp.zeros_like(acc)

    def one(n, _):
        v = lax.rem(n, 2)
        vals_copy(n).wait()

        def scatter(s, _):
            start = n * chunk + s * unroll
            for q in range(unroll):
                rows = [rows_ref[start + (k * part + q)] for k in range(len(accs))]
                news = [
                    acc[pl.ds(r, 1), :] + vbuf[v, pl.ds(s * unroll + (k * part + q), 1), :]
                    for k, (acc, r) in enumerate(zip(accs, rows))
                ]
                for acc, r, new in zip(accs, rows, news):
                    acc[pl.ds(r, 1), :] = new
            return 0

        lax.fori_loop(0, part // unroll, scatter, 0)

        @pl.when(n + 2 < chunks)
        def _():
            vals_copy(n + 2).start()

        return 0

    lax.fori_loop(0, chunks, one, 0)
    table_copy.wait()
    state_copy.wait()
    u0, u1 = split2(ugram_ref[...])
    u00 = jnp.concatenate([u0, u0], axis=0)

    def out_copy(t, which):
        at = pl.ds(pl.multiple_of(t * tile, 8), tile)
        src, dst = ((table, new_table_ref), (state, new_state_ref))[which]
        return pltpu.make_async_copy(src.at[at], dst.at[at], out_sem.at[which, t])

    def finish(t, _):
        at = pl.ds(pl.multiple_of(t * tile, 8), tile)
        item = table[at, :]
        t0, t1 = split2(item)
        g = jnp.dot(jnp.concatenate([t0, t1], axis=1), u00, preferred_element_type=f32)
        g = 2.0 * coef * (g + jnp.dot(t0, u1, preferred_element_type=f32))
        add = accs[0][at, :]
        for acc in accs[1:]:
            add = add + acc[at, :]
        g = g + add
        new = state[at, :] + g * g
        state[at, :] = new
        table[at, :] = item - step_size * g / jnp.sqrt(new)
        out_copy(t, 0).start()
        out_copy(t, 1).start()
        return 0

    lax.fori_loop(0, tiles, finish, 0)

    def drain(t, _):
        out_copy(t, 0).wait()
        out_copy(t, 1).wait()
        return 0

    lax.fori_loop(0, tiles, drain, 0)


VM = pl.BlockSpec(memory_space=pltpu.VMEM)
HB = pl.BlockSpec(memory_space=pl.ANY)
SM = pl.BlockSpec(memory_space=pltpu.SMEM)
PARAMS = pltpu.CompilerParams(vmem_limit_bytes=60 * 1024 * 1024)


def shards(item_table, adagrad_state, history_ids, positive_ids):
    rows_dev, width = item_table.shape
    users_dev, hist_len = history_ids.shape
    devices = lax.axis_size("dp") * lax.axis_size("rows")
    groups = 2 * users_dev
    count = users_dev * (hist_len + 1)
    capacity = max(8, (count * 5 // (2 * devices) + 7) // 8 * 8)
    block = 512
    padded = round_up(count, block)
    requests = jnp.concatenate([history_ids.reshape(-1), positive_ids])
    code = jnp.concatenate(
        [jnp.arange(users_dev * hist_len, dtype=i32) // hist_len, users_dev + jnp.arange(users_dev, dtype=i32)]
    )
    requests = jnp.pad(requests, (0, padded - count), constant_values=devices * rows_dev)
    code = jnp.pad(code, (0, padded - count))
    owner = requests // rows_dev
    local = requests - owner * rows_dev

    lists = pl.pallas_call(
        functools.partial(route_kernel, devices, capacity, users_dev, block),
        out_shape=jax.ShapeDtypeStruct((2, devices, capacity), i32),
        in_specs=[VM] * 3,
        out_specs=VM,
        scratch_shapes=[pltpu.VMEM((4 * devices, capacity), f32)],
        compiler_params=PARAMS,
        name="route",
    )(owner[None], local[None], code[None])
    asked = lax.all_to_all(lists, ("dp", "rows"), split_axis=1, concat_axis=1, tiled=True)
    rows = asked[0].reshape(-1)
    codes = asked[1]
    entries = devices * capacity
    item_gram = jnp.dot(item_table.T, item_table, precision=HIGHEST, preferred_element_type=f32)
    data, shard = lax.axis_size("dp"), lax.axis_size("rows")
    sizes = line_sizes(data, shard)
    plane = devices // 2
    lines = sum(sizes) - 1
    coef = penalty_weight / (rows_dev * devices)
    dma = pltpu.SemaphoreType.DMA
    vals, user_gram = pl.pallas_call(
        functools.partial(exchange_kernel, sizes, capacity, users_dev, hist_len, coef, 32),
        out_shape=(
            jax.ShapeDtypeStruct((devices, capacity, width), f32),
            jax.ShapeDtypeStruct((width, width), f32),
        ),
        in_specs=[SM, SM, VM, VM, VM],
        out_specs=(HB, VM),
        scratch_shapes=[
            pltpu.VMEM((capacity, width), f32),
            pltpu.VMEM((2, plane, 2, users_dev, width), f32),
            pltpu.VMEM((plane, 2, users_dev, width), f32),
            pltpu.VMEM((2, plane, users_dev, width), f32),
            pltpu.VMEM((devices, 2, users_dev, width), f32),
            pltpu.VMEM((groups + 8, width), f32),
            pltpu.VMEM((VSLOTS, capacity, width), f32),
            pltpu.VMEM((width, width), f32),
            pltpu.VMEM((2, 4, width // 2, width), f32),
            pltpu.VMEM((2, lines, width // 2, width), f32),
            pltpu.VMEM((2, width, width), f32),
            dma((plane,)),
            dma((plane,)),
            dma((2, plane)),
            dma((2, plane)),
            dma((2, plane)),
            dma((2, plane)),
            dma((plane,)),
            dma((plane,)),
            dma((2, lines)),
            dma((2, lines)),
            dma((VSLOTS,)),
        ],
        compiler_params=pltpu.CompilerParams(
            vmem_limit_bytes=60 * 1024 * 1024, collective_id=0, has_side_effects=True
        ),
        name="exchange",
    )(rows, codes.reshape(-1), codes[:, None, :], item_gram, item_table)
    chunk, tile = min(2048, entries), 256
    return pl.pallas_call(
        functools.partial(scatter_kernel, coef, chunk, 4, tile),
        out_shape=(
            jax.ShapeDtypeStruct(item_table.shape, f32),
            jax.ShapeDtypeStruct(item_table.shape, f32),
        ),
        in_specs=[SM, HB, VM, HB, HB],
        out_specs=(HB, HB),
        scratch_shapes=[
            pltpu.VMEM((2, chunk, width), f32),
            pltpu.VMEM((rows_dev, width), f32),
            pltpu.VMEM((rows_dev, width), f32),
            dma((2,)),
            dma((2,)),
            dma((2, rows_dev // tile)),
        ]
        + [pltpu.VMEM((rows_dev, width), f32)] * STREAMS,
        compiler_params=PARAMS,
        name="scatter",
    )(rows, vals.reshape(entries, width), user_gram, item_table, adagrad_state)


def solution(mesh):
    return jax.shard_map(
        shards,
        mesh=mesh,
        in_specs=(
            P(("dp", "rows"), None),
            P(("dp", "rows"), None),
            P(("dp", "rows"), None),
            P(("dp", "rows")),
        ),
        out_specs=(P(("dp", "rows"), None), P(("dp", "rows"), None)),
        check_vma=False,
    )
```

time: 217 us -> 138 us (0.64)
  the two profiles are of different devices: /device:TPU:29 before, /device:TPU:0 now
where the time goes in v1:
time: 138 us
  Pallas kernels  116 us (84%)
  starting transfers between devices  7.33 us (5%)
  matrix products  6.29 us (5%)
  local copies, waits for them, and re-layouts  5.31 us (4%)
  waiting for transfers between devices  1.51 us (1%)
    pallas_call x1, Pallas kernels, shards(): pl.pallas_call(functools.partial(exchange_kernel, sizes, capacity, users_...  84 us
    pallas_call x1, Pallas kernels, shards(): pl.pallas_call(functools.partial(scatter_kernel, coef, chunk, 4, tile), o...  25.6 us
    all_to_all x1, starting transfers between devices, shards(): lax.all_to_all(lists, ('dp', 'rows'), split_axis=1, concat_axis=1, tiled=...  7.33 us
    dot_general x1, matrix products, shards(): jnp.dot(item_table.T, item_table, precision=HIGHEST, preferred_element_ty...  6.29 us
    pallas_call x1, Pallas kernels, shards(): pl.pallas_call(functools.partial(route_kernel, devices, capacity, users_d...  6.13 us
  transfers between devices with their start and end apart: 1, of which 1 were waited for; matrix products, arithmetic and copies ran while one was open for 5% of the time, Pallas kernels for 0%

profile of v1, /device:TPU:0, one launch (start us, length us, event | category | flops | bytes accessed | tf_op | source)
XLA Modules:
  0.0 137.5 jit_solution(17173069142667413557)
XLA Ops:
  0.7 0.6 broadcast_in_dim.11.code_ref
  1.3 0.8 copy.7
  2.2 0.1 reshape.10
  2.3 0.7 pad_add_fusion
  3.0 0.6 broadcast_in_dim.10.local_ref
  3.6 0.6 broadcast_in_dim.9.owner_ref
  4.2 6.1 %route.1 = s32[2,32,512]{2,1,0:T(8,128)} custom-call(s32[1,6656]{1,0:T(1,128)} %broadcast_in_dim.9.owner_ref, s32[1,6656]{1,0:T(1,128)} %broadcast_in_dim.10.local_ref, s32[1,6656]{1,0:T(1,128)} %broadcast_in_dim.11.code_ref), custom_call_target="tpu_custom_call" | custom-call | tf_op jit(solution)/shard_map/route/pallas_call | solution.py:523
  10.4 1.7 %copy.8 = s32[2,32,512]{2,0,1:T(2,128)} copy(s32[2,32,512]{2,1,0:T(8,128)} %route.1) | data formatting | bytes 262144 | tf_op jit(solution)/shard_map/route/pallas_call | solution.py:523
  12.0 7.3 %all-to-all-start = ((s32[2,32,512]{2,0,1:T(2,128)}), s32[2,32,512]{2,0,1:T(2,128)S(1)}, u32[]{:S(2)}, u32[]{:S(2)}) async-start(s32[2,32,512]{2,0,1:T(2,128)} %copy.8), calls=%async_computation | async-start | bytes 262144 | tf_op jit(solution)/shard_map/all_to_all | solution.py:532
  19.4 6.3 %fusion.5.gram_ref = f32[128,128]{1,0:T(8,128)} fusion(f32[4096,128]{1,0:T(8,128)} %table_ref.3), kind=kOutput, calls=%fused_computation.19 | convolution fusion | flops 805306368 | bytes 2162688 | tf_op jit(solution)/shard_map/dot_general | solution.py:536
  25.7 1.5 %all-to-all-done = s32[2,32,512]{2,0,1:T(2,128)S(1)} async-done(((s32[2,32,512]{2,0,1:T(2,128)}), s32[2,32,512]{2,0,1:T(2,128)S(1)}, u32[]{:S(2)}, u32[]{:S(2)}) %all-to-all-start) | async-done | bytes 131104 | tf_op jit(solution)/shard_map/all_to_all | solution.py:532
  27.2 0.8 slice_bitcast_fusion
  28.0 84.0 %exchange.1 = (f32[32,512,128]{2,1,0:T(8,128)}, f32[128,128]{1,0:T(8,128)}) custom-call(s32[16384]{0:T(1024)} %bitcast.8, s32[16384]{0:T(1024)} %bitcast.10, s32[32,1,512]{2,1,0:T(1,128)} %get-tuple-element.6.hot_ref, f32[128,128]{1,0:T(8,128)} %fusion.5.gram_ref, f32[4096,128]{1,0:T(8,128)} %table_ref.3), custom_call_target="tpu_custom_call" | custom-call | tf_op jit(solution)/shard_map/exchange/pallas_call | solution.py:543
  111.9 25.6 %scatter.1 = (f32[4096,128]{1,0:T(8,128)}, f32[4096,128]{1,0:T(8,128)}) custom-call(s32[16384]{0:T(1024)} %bitcast.9, f32[16384,128]{1,0:T(8,128)} %bitcast.7, f32[128,128]{1,0:T(8,128)} %get-tuple-element.5.ugram_ref, f32[4096,128]{1,0:T(8,128)} %table_ref.3, f32[4096,128]{1,0:T(8,128)} %state_ref.1), custom_call_target="tpu_custom_call" | custom-call | tf_op jit(solution)/shard_map/scatter/pallas_call | solution.py:581
  (5 shorter events, 0.1 us)
Async XLA Ops:
  12.0 15.1 %all-to-all-start = ((s32[2,32,512]{2,0,1:T(2,128)}), s32[2,32,512]{2,0,1:T(2,128)S(1)}, u32[]{:S(2)}, u32[]{:S(2)}) async-start(s32[2,32,512]{2,0,1:T(2,128)} %copy.8), calls=%async_computation | async-start | bytes 262144 | tf_op jit(solution)/shard_map/all_to_all | solution.py:532

commit v2 on v1

--- a/solution.py
+++ b/solution.py
@@ -63,9 +63,10 @@
     return data // 2, cols, shard // cols
 
 
-ORDERS = ((0, 1, 2), (1, 2, 0))
-LAGS = (2, 4, 6, 8)
+ORDERS = ((0, 1, 2), (1, 0, 2))
+LAGS = (2, 3, 4, 5)
 VSLOTS = 4
+TWIN_LAG = 1
 
 
 def exchange_kernel(
@@ -107,8 +108,12 @@
     def slot(r):
         return (r[0] * ny + r[1]) * nz + r[2]
 
-    def unslot(at):
-        return at // (ny * nz), lax.rem(at // nz, ny), lax.rem(at, nz)
+    def ranked(n, digits):
+        out = [0, 0, 0]
+        for a in reversed(digits):
+            out[a] = lax.rem(n, sizes[a])
+            n = n // sizes[a]
+        return tuple(out)
 
     partner = device(pos, 1 - core)
 
@@ -208,7 +213,7 @@
         def some(s, _):
             start = base + s * unroll
             for k in range(unroll):
-                r = rows_ref[start + k]
+                r = rows_ref.at[pl.ds(k, rows_ref.shape[0] - unroll + 1)][start]
                 picked[pl.ds(s * unroll + k, 1), :] = table_ref[pl.ds(r, 1), :]
             return 0
 
@@ -239,11 +244,11 @@
     def reduce_step(i, _):
         for stage in range(4):
             j = i - LAGS[stage]
-            at = plane - 1 - j
 
             @pl.when(jnp.logical_and(j >= 0, j < plane))
             def _():
-                r = unslot(at)
+                r = ranked(plane - 1 - j, (2, 0, 1))
+                at = slot(r)
                 if stage == 0:
                     pair_copy(at).wait_recv()
                     for h in range(2):
@@ -269,8 +274,9 @@
 
         @pl.when(i < plane)
         def _():
-            at = plane - 1 - i
-            chip = ahead(unslot(at))
+            r = ranked(plane - 1 - i, (2, 0, 1))
+            at = slot(r)
+            chip = ahead(r)
 
             def one(j, _):
                 c = (1 - core) * (1 - j) + core * j
@@ -300,11 +306,6 @@
         for k in range(1, sizes[a]):
             chip = tuple(lax.rem(p + k, n) if c == a else p for c, (p, n) in enumerate(zip(pos, sizes)))
             parcel(h, slot(add(o, a, k)), b, device(chip, core)).start()
-
-    def received(h, o):
-        b = block(behind(o), core)
-        parcel(h, slot(o), b, partner).wait_recv()
-        return b
 
     ways = tuple(order[::-1] for order in ORDERS)
     for a in range(3):
@@ -320,10 +321,10 @@
     def vals_copy(v, b):
         return pltpu.make_async_copy(vbuf.at[v], vals_ref.at[b], vsem.at[v])
 
-    def vals(n, b):
-        v = lax.rem(n, VSLOTS)
-
-        @pl.when(n >= VSLOTS)
+    def vals(n, kind, b):
+        v = 2 * kind + lax.rem(n, 2)
+
+        @pl.when(n >= 2)
         def _():
             vals_copy(v, b).wait()
 
@@ -334,61 +335,72 @@
         def some(s, _):
             start = base + s * unroll
             for k in range(unroll):
-                c = codes_ref[start + k]
+                c = codes_ref.at[pl.ds(k, codes_ref.shape[0] - unroll + 1)][start]
                 vbuf[v, pl.ds(s * unroll + k, 1), :] = cur[pl.ds(c, 1), :]
             return 0
 
         lax.fori_loop(0, capacity // unroll, some, 0)
         vals_copy(v, b).start()
 
-    for h in range(2):
-        a1, a2, a3 = ways[h]
-        for k in range(1, sizes[a1]):
-            o = only(a1, k)
-            b = received(h, o)
-            forward(h, o, b, a2)
-            forward(h, o, b, a3)
-    gram_step(1, upart, 0)
-    for h in range(2):
-        a1, a2, a3 = ways[h]
-        for k in range(1, sizes[a2]):
-            for m in range(sizes[a1]):
-                o = add(only(a2, k), a1, m)
-                b = received(h, o)
-                forward(h, o, b, a3)
-        gram_step(1, upart, h + 1)
+    seqs = tuple(way[::-1] for way in ways)
+
+    def rank(o, digits):
+        n = 0
+        for a in digits:
+            n = n * sizes[a] + o[a]
+        return n
+
+    chips = [(x, y, z) for x in range(nx) for y in range(ny) for z in range(nz)]
+    lag = 1 + max(rank(o, seqs[h]) - rank(o, seqs[0]) for o in chips for h in range(2))
 
     def spread(n, _):
-        @pl.when(n < plane)
+        def one(kind, _):
+            j = n - lag - TWIN_LAG * kind
+
+            @pl.when(jnp.logical_and(j >= 0, j < plane))
+            def _():
+                o = ranked(j, seqs[0])
+                at = slot(o)
+                b = block(behind(o), core + kind * (1 - 2 * core))
+
+                @pl.when(jnp.logical_and(kind == 0, j > 0))
+                def _():
+                    twin(at, b).start()
+
+                @pl.when(kind == 1)
+                def _():
+                    twin(at, b).wait_recv()
+
+                vals(j, kind, b)
+
+            return 0
+
+        lax.fori_loop(0, 2, one, 0)
+
+        @pl.when(jnp.logical_and(n > 0, n < plane))
         def _():
-            o = unslot(n)
-            b = block(behind(o), core)
             for h in range(2):
-                @pl.when(o[ways[h][2]] != 0)
+                a1, a2, a3 = ways[h]
+                o = ranked(n, seqs[h])
+                b = block(behind(o), core)
+                parcel(h, slot(o), b, partner).wait_recv()
+
+                @pl.when(o[a3] == 0)
                 def _():
-                    received(h, o)
-
-            @pl.when(n > 0)
-            def _():
-                twin(n, b).start()
-
-            vals(2 * n, b)
-
-        @pl.when(n > 0)
-        def _():
-            o = unslot(n - 1)
-            b = block(behind(o), 1 - core)
-            twin(n - 1, b).wait_recv()
-            vals(2 * n - 1, b)
-
-        for stage in (3, 4):
-            @pl.when(n == 4 * (stage - 2))
+                    @pl.when(o[a2] == 0)
+                    def _():
+                        forward(h, o, b, a2)
+
+                    forward(h, o, b, a3)
+
+        for stage in range(5):
+            @pl.when(n == 2 * stage + 2)
             def _():
                 gram_step(1, upart, stage)
 
         return 0
 
-    lax.fori_loop(0, plane + 1, spread, 0)
+    lax.fori_loop(0, plane + lag + TWIN_LAG, spread, 0)
     ugram_ref[...] = gfull[1]
 
     def drain(n):
@@ -441,7 +453,9 @@
         def scatter(s, _):
             start = n * chunk + s * unroll
             for q in range(unroll):
-                rows = [rows_ref[start + (k * part + q)] for k in range(len(accs))]
+                rows = [
+                    rows_ref.at[pl.ds(k * part + q, entries - chunk + part - unroll + 1)][start] for k in range(len(accs))
+                ]
                 news = [
                     acc[pl.ds(r, 1), :] + vbuf[v, pl.ds(s * unroll + (k * part + q), 1), :]
                     for k, (acc, r) in enumerate(zip(accs, rows))
@@ -538,10 +552,11 @@
     sizes = line_sizes(data, shard)
     plane = devices // 2
     lines = sum(sizes) - 1
+    unroll = max(n for n in (8, 16, 32, 64, 128) if capacity % n == 0)
     coef = penalty_weight / (rows_dev * devices)
     dma = pltpu.SemaphoreType.DMA
     vals, user_gram = pl.pallas_call(
-        functools.partial(exchange_kernel, sizes, capacity, users_dev, hist_len, coef, 32),
+        functools.partial(exchange_kernel, sizes, capacity, users_dev, hist_len, coef, unroll),
         out_shape=(
             jax.ShapeDtypeStruct((devices, capacity, width), f32),
             jax.ShapeDtypeStruct((width, width), f32),

time: 138 us -> 130 us (0.942)
  Pallas kernels: 116 us -> 108 us
    pallas_call x1, Pallas kernels: 84 us -> 75.8 us  [shards(): pl.pallas_call(functools.partial(exchange_kernel, sizes, capacity, users_...]
where the time goes in v2:
time: 130 us
  Pallas kernels  108 us (83%)
  starting transfers between devices  7.33 us (6%)
  matrix products  6.29 us (5%)
  local copies, waits for them, and re-layouts  5.31 us (4%)
  waiting for transfers between devices  1.51 us (1%)
    pallas_call x1, Pallas kernels, shards(): pl.pallas_call(functools.partial(exchange_kernel, sizes, capacity, users_...  75.8 us
    pallas_call x1, Pallas kernels, shards(): pl.pallas_call(functools.partial(scatter_kernel, coef, chunk, 4, tile), o...  26 us
    all_to_all x1, starting transfers between devices, shards(): lax.all_to_all(lists, ('dp', 'rows'), split_axis=1, concat_axis=1, tiled=...  7.33 us
    dot_general x1, matrix products, shards(): jnp.dot(item_table.T, item_table, precision=HIGHEST, preferred_element_ty...  6.29 us
    pallas_call x1, Pallas kernels, shards(): pl.pallas_call(functools.partial(route_kernel, devices, capacity, users_d...  6.13 us
  transfers between devices with their start and end apart: 1, of which 1 were waited for; matrix products, arithmetic and copies ran while one was open for 5% of the time, Pallas kernels for 0%

profile of v2, /device:TPU:0, one launch (start us, length us, event | category | flops | bytes accessed | tf_op | source)
XLA Modules:
  0.0 129.7 jit_solution(8221111087125392990)
XLA Ops:
  0.7 0.6 broadcast_in_dim.11.code_ref
  1.3 0.8 copy.7
  2.2 0.1 reshape.10
  2.3 0.7 pad_add_fusion
  3.0 0.6 broadcast_in_dim.10.local_ref
  3.6 0.6 broadcast_in_dim.9.owner_ref
  4.2 6.1 %route.1 = s32[2,32,512]{2,1,0:T(8,128)} custom-call(s32[1,6656]{1,0:T(1,128)} %broadcast_in_dim.9.owner_ref, s32[1,6656]{1,0:T(1,128)} %broadcast_in_dim.10.local_ref, s32[1,6656]{1,0:T(1,128)} %broadcast_in_dim.11.code_ref), custom_call_target="tpu_custom_call" | custom-call | tf_op jit(solution)/shard_map/route/pallas_call | solution.py:537
  10.4 1.7 %copy.8 = s32[2,32,512]{2,0,1:T(2,128)} copy(s32[2,32,512]{2,1,0:T(8,128)} %route.1) | data formatting | bytes 262144 | tf_op jit(solution)/shard_map/route/pallas_call | solution.py:537
  12.0 7.3 %all-to-all-start = ((s32[2,32,512]{2,0,1:T(2,128)}), s32[2,32,512]{2,0,1:T(2,128)S(1)}, u32[]{:S(2)}, u32[]{:S(2)}) async-start(s32[2,32,512]{2,0,1:T(2,128)} %copy.8), calls=%async_computation | async-start | bytes 262144 | tf_op jit(solution)/shard_map/all_to_all | solution.py:546
  19.4 6.3 %fusion.5.gram_ref = f32[128,128]{1,0:T(8,128)} fusion(f32[4096,128]{1,0:T(8,128)} %table_ref.3), kind=kOutput, calls=%fused_computation.19 | convolution fusion | flops 805306368 | bytes 2162688 | tf_op jit(solution)/shard_map/dot_general | solution.py:550
  25.7 1.5 %all-to-all-done = s32[2,32,512]{2,0,1:T(2,128)S(1)} async-done(((s32[2,32,512]{2,0,1:T(2,128)}), s32[2,32,512]{2,0,1:T(2,128)S(1)}, u32[]{:S(2)}, u32[]{:S(2)}) %all-to-all-start) | async-done | bytes 131104 | tf_op jit(solution)/shard_map/all_to_all | solution.py:546
  27.2 0.8 slice_bitcast_fusion
  28.0 75.8 %exchange.1 = (f32[32,512,128]{2,1,0:T(8,128)}, f32[128,128]{1,0:T(8,128)}) custom-call(s32[16384]{0:T(1024)} %bitcast.8, s32[16384]{0:T(1024)} %bitcast.10, s32[32,1,512]{2,1,0:T(1,128)} %get-tuple-element.6.hot_ref, f32[128,128]{1,0:T(8,128)} %fusion.5.gram_ref, f32[4096,128]{1,0:T(8,128)} %table_ref.3), custom_call_target="tpu_custom_call" | custom-call | tf_op jit(solution)/shard_map/exchange/pallas_call | solution.py:558
  103.7 26.0 %scatter.1 = (f32[4096,128]{1,0:T(8,128)}, f32[4096,128]{1,0:T(8,128)}) custom-call(s32[16384]{0:T(1024)} %bitcast.9, f32[16384,128]{1,0:T(8,128)} %bitcast.7, f32[128,128]{1,0:T(8,128)} %get-tuple-element.5.ugram_ref, f32[4096,128]{1,0:T(8,128)} %table_ref.3, f32[4096,128]{1,0:T(8,128)} %state_ref.1), custom_call_target="tpu_custom_call" | custom-call | tf_op jit(solution)/shard_map/scatter/pallas_call | solution.py:596
  (5 shorter events, 0.1 us)
Async XLA Ops:
  12.0 15.1 %all-to-all-start = ((s32[2,32,512]{2,0,1:T(2,128)}), s32[2,32,512]{2,0,1:T(2,128)S(1)}, u32[]{:S(2)}, u32[]{:S(2)}) async-start(s32[2,32,512]{2,0,1:T(2,128)} %copy.8), calls=%async_computation | async-start | bytes 262144 | tf_op jit(solution)/shard_map/all_to_all | solution.py:546

commit v3 on v2

--- a/solution.py
+++ b/solution.py
@@ -64,9 +64,9 @@
 
 
 ORDERS = ((0, 1, 2), (1, 0, 2))
-LAGS = (2, 3, 4, 5)
+LAGS = (2, 4, 6, 8)
 VSLOTS = 4
-TWIN_LAG = 1
+TWIN_LAG = 2
 
 
 def exchange_kernel(
@@ -268,7 +268,7 @@
                                 leave(h, r, order[stage])
 
         for stage in range(5):
-            @pl.when(i == 2 * stage + 2)
+            @pl.when(i == 3 * stage + 3)
             def _():
                 gram_step(0, gram_ref, stage)
 
@@ -308,7 +308,11 @@
             parcel(h, slot(add(o, a, k)), b, device(chip, core)).start()
 
     ways = tuple(order[::-1] for order in ORDERS)
-    for a in range(3):
+    line = ways[0][0]
+    for k in range(1, sizes[line]):
+        for h in range(2):
+            parcel(h, slot(only(line, k)), me, device(ahead(only(line, k)), core)).start()
+    for a in (1, 2):
         for h in range(2):
             forward(h, origin, me, ways[h][a])
     twin(0, me).start()
@@ -342,24 +346,36 @@
         lax.fori_loop(0, capacity // unroll, some, 0)
         vals_copy(v, b).start()
 
-    seqs = tuple(way[::-1] for way in ways)
-
-    def rank(o, digits):
-        n = 0
-        for a in digits:
-            n = n * sizes[a] + o[a]
-        return n
-
-    chips = [(x, y, z) for x in range(nx) for y in range(ny) for z in range(nz)]
-    lag = 1 + max(rank(o, seqs[h]) - rank(o, seqs[0]) for o in chips for h in range(2))
+    digits = ((2, 0, 1), (2, 1, 0))
+    delays = (-nx * ny, 1, 3)
+    vals_delay = delays[2] + 1
 
     def spread(n, _):
+        for h in range(2):
+            a1, a2, a3 = ways[h]
+            for level in (1, 2, 3):
+                q = n - delays[level - 1]
+                o = ranked(q, digits[h])
+                if level == 1:
+                    here = jnp.logical_and(o[a1] != 0, jnp.logical_and(o[a2] == 0, o[a3] == 0))
+                elif level == 2:
+                    here = jnp.logical_and(o[a2] != 0, o[a3] == 0)
+                else:
+                    here = o[a3] != 0
+
+                @pl.when(jnp.logical_and(jnp.logical_and(q >= 0, q < plane), here))
+                def _():
+                    b = block(behind(o), core)
+                    parcel(h, slot(o), b, partner).wait_recv()
+                    for a in ways[h][level:]:
+                        forward(h, o, b, a)
+
         def one(kind, _):
-            j = n - lag - TWIN_LAG * kind
+            j = n - vals_delay - TWIN_LAG * kind
 
             @pl.when(jnp.logical_and(j >= 0, j < plane))
             def _():
-                o = ranked(j, seqs[0])
+                o = ranked(j, digits[0])
                 at = slot(o)
                 b = block(behind(o), core + kind * (1 - 2 * core))
 
@@ -377,30 +393,14 @@
 
         lax.fori_loop(0, 2, one, 0)
 
-        @pl.when(jnp.logical_and(n > 0, n < plane))
-        def _():
-            for h in range(2):
-                a1, a2, a3 = ways[h]
-                o = ranked(n, seqs[h])
-                b = block(behind(o), core)
-                parcel(h, slot(o), b, partner).wait_recv()
-
-                @pl.when(o[a3] == 0)
-                def _():
-                    @pl.when(o[a2] == 0)
-                    def _():
-                        forward(h, o, b, a2)
-
-                    forward(h, o, b, a3)
-
         for stage in range(5):
-            @pl.when(n == 2 * stage + 2)
+            @pl.when(n == 4 * stage + 3)
             def _():
                 gram_step(1, upart, stage)
 
         return 0
 
-    lax.fori_loop(0, plane + lag + TWIN_LAG, spread, 0)
+    lax.fori_loop(0, plane + vals_delay + TWIN_LAG, spread, 0)
     ugram_ref[...] = gfull[1]
 
     def drain(n):

time: 130 us -> 118 us (0.908)
  Pallas kernels: 108 us -> 95.9 us
    pallas_call x1, Pallas kernels: 75.8 us -> 64.2 us  [shards(): pl.pallas_call(functools.partial(exchange_kernel, sizes, capacity, users_...]
where the time goes in v3:
time: 118 us
  Pallas kernels  95.9 us (81%)
  starting transfers between devices  7.33 us (6%)
  matrix products  6.29 us (5%)
  local copies, waits for them, and re-layouts  5.31 us (4%)
  waiting for transfers between devices  1.51 us (1%)
    pallas_call x1, Pallas kernels, shards(): pl.pallas_call(functools.partial(exchange_kernel, sizes, capacity, users_...  64.2 us
    pallas_call x1, Pallas kernels, shards(): pl.pallas_call(functools.partial(scatter_kernel, coef, chunk, 4, tile), o...  25.6 us
    all_to_all x1, starting transfers between devices, shards(): lax.all_to_all(lists, ('dp', 'rows'), split_axis=1, concat_axis=1, tiled=...  7.33 us
    dot_general x1, matrix products, shards(): jnp.dot(item_table.T, item_table, precision=HIGHEST, preferred_element_ty...  6.29 us
    pallas_call x1, Pallas kernels, shards(): pl.pallas_call(functools.partial(route_kernel, devices, capacity, users_d...  6.13 us
  transfers between devices with their start and end apart: 1, of which 1 were waited for; matrix products, arithmetic and copies ran while one was open for 5% of the time, Pallas kernels for 0%

profile of v3, /device:TPU:0, one launch (start us, length us, event | category | flops | bytes accessed | tf_op | source)
XLA Modules:
  0.0 117.8 jit_solution(7079285186470813421)
XLA Ops:
  0.7 0.6 broadcast_in_dim.11.code_ref
  1.3 0.8 copy.7
  2.2 0.1 reshape.10
  2.3 0.7 pad_add_fusion
  3.0 0.6 broadcast_in_dim.10.local_ref
  3.6 0.6 broadcast_in_dim.9.owner_ref
  4.2 6.1 %route.1 = s32[2,32,512]{2,1,0:T(8,128)} custom-call(s32[1,6656]{1,0:T(1,128)} %broadcast_in_dim.9.owner_ref, s32[1,6656]{1,0:T(1,128)} %broadcast_in_dim.10.local_ref, s32[1,6656]{1,0:T(1,128)} %broadcast_in_dim.11.code_ref), custom_call_target="tpu_custom_call" | custom-call | tf_op jit(solution)/shard_map/route/pallas_call | solution.py:537
  10.4 1.7 %copy.8 = s32[2,32,512]{2,0,1:T(2,128)} copy(s32[2,32,512]{2,1,0:T(8,128)} %route.1) | data formatting | bytes 262144 | tf_op jit(solution)/shard_map/route/pallas_call | solution.py:537
  12.0 7.3 %all-to-all-start = ((s32[2,32,512]{2,0,1:T(2,128)}), s32[2,32,512]{2,0,1:T(2,128)S(1)}, u32[]{:S(2)}, u32[]{:S(2)}) async-start(s32[2,32,512]{2,0,1:T(2,128)} %copy.8), calls=%async_computation | async-start | bytes 262144 | tf_op jit(solution)/shard_map/all_to_all | solution.py:546
  19.4 6.3 %fusion.5.gram_ref = f32[128,128]{1,0:T(8,128)} fusion(f32[4096,128]{1,0:T(8,128)} %table_ref.3), kind=kOutput, calls=%fused_computation.19 | convolution fusion | flops 805306368 | bytes 2162688 | tf_op jit(solution)/shard_map/dot_general | solution.py:550
  25.7 1.5 %all-to-all-done = s32[2,32,512]{2,0,1:T(2,128)S(1)} async-done(((s32[2,32,512]{2,0,1:T(2,128)}), s32[2,32,512]{2,0,1:T(2,128)S(1)}, u32[]{:S(2)}, u32[]{:S(2)}) %all-to-all-start) | async-done | bytes 131104 | tf_op jit(solution)/shard_map/all_to_all | solution.py:546
  27.2 0.8 slice_bitcast_fusion
  28.0 64.2 %exchange.1 = (f32[32,512,128]{2,1,0:T(8,128)}, f32[128,128]{1,0:T(8,128)}) custom-call(s32[16384]{0:T(1024)} %bitcast.8, s32[16384]{0:T(1024)} %bitcast.10, s32[32,1,512]{2,1,0:T(1,128)} %get-tuple-element.6.hot_ref, f32[128,128]{1,0:T(8,128)} %fusion.5.gram_ref, f32[4096,128]{1,0:T(8,128)} %table_ref.3), custom_call_target="tpu_custom_call" | custom-call | tf_op jit(solution)/shard_map/exchange/pallas_call | solution.py:558
  92.1 25.6 %scatter.1 = (f32[4096,128]{1,0:T(8,128)}, f32[4096,128]{1,0:T(8,128)}) custom-call(s32[16384]{0:T(1024)} %bitcast.9, f32[16384,128]{1,0:T(8,128)} %bitcast.7, f32[128,128]{1,0:T(8,128)} %get-tuple-element.5.ugram_ref, f32[4096,128]{1,0:T(8,128)} %table_ref.3, f32[4096,128]{1,0:T(8,128)} %state_ref.1), custom_call_target="tpu_custom_call" | custom-call | tf_op jit(solution)/shard_map/scatter/pallas_call | solution.py:596
  (5 shorter events, 0.1 us)
Async XLA Ops:
  12.0 15.1 %all-to-all-start = ((s32[2,32,512]{2,0,1:T(2,128)}), s32[2,32,512]{2,0,1:T(2,128)S(1)}, u32[]{:S(2)}, u32[]{:S(2)}) async-start(s32[2,32,512]{2,0,1:T(2,128)} %copy.8), calls=%async_computation | async-start | bytes 262144 | tf_op jit(solution)/shard_map/all_to_all | solution.py:546

commit v4 on v3

--- a/solution.py
+++ b/solution.py
@@ -19,45 +19,135 @@
     return (value + unit - 1) // unit * unit
 
 
-def route_kernel(devices, capacity, users_dev, block, owner_ref, local_ref, code_ref, out_ref, acc):
-    blocks = owner_ref.shape[1] // block
-    upper = (
-        lax.broadcasted_iota(i32, (block, block), 0) <= lax.broadcasted_iota(i32, (block, block), 1)
-    ).astype(bf16)
-    owners = lax.broadcasted_iota(i32, (devices, block), 0)
-    ranks_to = lax.broadcasted_iota(i32, (capacity, block), 0)
-    acc[...] = jnp.zeros_like(acc)
-    carry = jnp.zeros((devices, 1), f32)
-    for j in range(blocks):
-        cols = slice(j * block, (j + 1) * block)
-        local = local_ref[:, cols]
-        high = (local // LOW).astype(f32)
-        low = (local % LOW).astype(f32)
-        code = code_ref[:, cols].astype(f32)
-        member = (owner_ref[:, cols] == owners).astype(f32)
-        prefix = jnp.dot(member.astype(bf16), upper, preferred_element_type=f32)
-        rank = jnp.sum(member * (prefix + carry), axis=0, keepdims=True) - 1.0
-        carry = carry + jnp.sum(member, axis=1, keepdims=True)
-        left = jnp.concatenate(
-            [member * high, member * low, member * code, member], axis=0
-        ).astype(bf16)
-        right = (rank.astype(i32) == ranks_to).astype(f32).astype(bf16)
-        acc[...] += lax.dot_general(
-            left, right, (((1,), (1,)), ((), ())), preferred_element_type=f32
-        )
-    row = acc[0:devices] * LOW + acc[devices : 2 * devices]
-    code = acc[2 * devices : 3 * devices]
-    present = acc[3 * devices : 4 * devices]
-    empty = 2 * users_dev
-    out_ref[0] = row.astype(i32)
-    out_ref[1] = jnp.where(present > 0.5, code, float(empty)).astype(i32)
-
-
 def split2(x):
     hi = x.astype(bf16)
     return hi, (x - hi.astype(f32)).astype(bf16)
 
 
+def ask_kernel(
+    data, shard, capacity, hist_ref, pos_ref, item_ref, rows_ref, codes_ref, gram_ref,
+    ids, acc, rows, codes, table_ref, row_send, row_recv, code_send, code_recv, own_sem,
+):
+    devices = data * shard
+    hist_len, users_dev = hist_ref.shape
+    width = item_ref.shape[1]
+    dp, rw = lax.axis_index("dp"), lax.axis_index("rows")
+
+    def each(first, count, act):
+        def step(k, _):
+            act(k)
+            return 0
+
+        lax.fori_loop(first, count, step, 0)
+
+    me = dp * shard + rw
+    rows_dev = item_ref.shape[0]
+    item_copy = pltpu.make_async_copy(item_ref, table_ref, own_sem.at[2])
+    item_copy.start()
+    barrier = pltpu.get_barrier_semaphore()
+
+    def place(n):
+        return n // shard, lax.rem(n, shard)
+
+    def greet(k):
+        pl.semaphore_signal(
+            barrier, inc=1, device_id=place(lax.rem(me + k, devices)), device_id_type=pl.DeviceIdType.MESH
+        )
+
+    each(1, devices, greet)
+    asks = ids.shape[0]
+    ids[0:hist_len, :] = hist_ref[...]
+    ids[hist_len : hist_len + 1, :] = pos_ref[...]
+    if asks > hist_len + 1:
+        ids[hist_len + 1 :, :] = jnp.full((asks - hist_len - 1, users_dev), devices * rows_dev, i32)
+    wide = ROWS_AT_ONCE * users_dev
+    upper = (
+        lax.broadcasted_iota(i32, (wide, wide), 0) <= lax.broadcasted_iota(i32, (wide, wide), 1)
+    ).astype(bf16)
+    owners = lax.broadcasted_iota(i32, (devices, wide), 0)
+    ranks_to = lax.broadcasted_iota(i32, (capacity, wide), 0)
+    lane = lax.broadcasted_iota(i32, (1, users_dev), 1)
+    acc[...] = jnp.zeros_like(acc)
+
+    def route(j, carry):
+        parts = [ids[pl.ds(j * ROWS_AT_ONCE + q, 1), :] for q in range(ROWS_AT_ONCE)]
+        codes = [
+            (lane + jnp.where(j * ROWS_AT_ONCE + q >= hist_len, users_dev, 0)).astype(f32)
+            for q in range(ROWS_AT_ONCE)
+        ]
+        want = jnp.concatenate(parts, axis=1)
+        code = jnp.concatenate(codes, axis=1)
+        owner = want // rows_dev
+        local = want - owner * rows_dev
+        high = (local // LOW).astype(f32)
+        low = (local % LOW).astype(f32)
+        member = (owner == owners).astype(f32)
+        prefix = jnp.dot(member.astype(bf16), upper, preferred_element_type=f32)
+        rank = jnp.sum(member * (prefix + carry), axis=0, keepdims=True) - 1.0
+        left = jnp.concatenate([member * high, member * low, member * code, member], axis=0).astype(bf16)
+        right = (rank.astype(i32) == ranks_to).astype(f32).astype(bf16)
+        acc[...] += lax.dot_general(left, right, (((1,), (1,)), ((), ())), preferred_element_type=f32)
+        return carry + jnp.sum(member, axis=1, keepdims=True)
+
+    lax.fori_loop(0, asks // ROWS_AT_ONCE, route, jnp.zeros((devices, 1), f32))
+
+    def write(d):
+        row = acc[pl.ds(d, 1), :] * LOW + acc[pl.ds(devices + d, 1), :]
+        code = acc[pl.ds(2 * devices + d, 1), :]
+        present = acc[pl.ds(3 * devices + d, 1), :]
+        rows[d] = row.astype(i32)
+        codes[d] = jnp.where(present > 0.5, code, 2.0 * users_dev).astype(i32)
+
+    each(0, devices, write)
+    pl.semaphore_wait(barrier, devices - 1)
+
+    def list_copies(k, to, at):
+        return tuple(
+            pltpu.make_async_remote_copy(
+                src_ref=src.at[to], dst_ref=dst.at[at], send_sem=send.at[k], recv_sem=recv.at[k],
+                device_id=place(to), device_id_type=pl.DeviceIdType.MESH,
+            )
+            for src, dst, send, recv in (
+                (rows, rows_ref, row_send, row_recv),
+                (codes, codes_ref, code_send, code_recv),
+            )
+        )
+
+    def send_list(k):
+        for copy in list_copies(k, lax.rem(me + k, devices), me):
+            copy.start()
+
+    each(1, devices, send_list)
+    own = (
+        pltpu.make_async_copy(rows.at[me], rows_ref.at[me], own_sem.at[0]),
+        pltpu.make_async_copy(codes.at[me], codes_ref.at[me], own_sem.at[1]),
+    )
+    for copy in own:
+        copy.start()
+    item_copy.wait()
+    tall = 512
+    gram_ref[...] = jnp.zeros_like(gram_ref)
+
+    def square(n):
+        hi, lo = split2(table_ref[pl.ds(pl.multiple_of(n * tall, 8), tall), :])
+        both = lax.dot_general(
+            hi, jnp.concatenate([hi, lo], axis=1), (((0,), (0,)), ((), ())), preferred_element_type=f32
+        )
+        gram_ref[...] += both[:, :width] + (both[:, width:] + both[:, width:].T)
+
+    each(0, rows_dev // tall, square)
+
+    def finish(k):
+        n = lax.rem(me - k + devices, devices)
+        for copy in list_copies(k, n, n):
+            copy.wait_recv()
+            copy.wait_send()
+
+    each(1, devices, finish)
+    for copy in own:
+        copy.wait()
+
+
 def line_sizes(data, shard):
     cols = max(n for n in range(1, shard + 1) if shard % n == 0 and n * n <= shard)
     return data // 2, cols, shard // cols
@@ -66,19 +156,20 @@
 ORDERS = ((0, 1, 2), (1, 0, 2))
 LAGS = (2, 4, 6, 8)
 VSLOTS = 4
+ROWS_AT_ONCE = 4
 TWIN_LAG = 2
 
 
 def exchange_kernel(
     sizes, capacity, users_dev, hist_len, coef, unroll,
-    rows_ref, codes_ref, hot_ref, gram_ref, table_ref, vals_ref, ugram_ref,
-    picked, part, pair, mail, grads, cur, vbuf, upart, gsum, gmail, gfull,
+    rows_hbm, codes_hbm, hot_ref, gram_ref, item_ref, vals_ref, ugram_ref,
+    rows_ref, codes_ref, table_ref, fetch_sem, picked, part, pair, mail, grads, cur, vbuf, upart, gsum, gmail, gfull,
     pair_send, pair_recv, mail_send, mail_recv, ag_send, ag_recv, twin_send, twin_recv, gram_send, gram_recv, vsem,
 ):
     nx, ny, nz = sizes
     plane = nx * ny * nz
     shard = ny * nz
-    width = table_ref.shape[1]
+    width = item_ref.shape[1]
     half = width // 2
     dp, rw = lax.axis_index("dp"), lax.axis_index("rows")
     core = lax.rem(dp, 2)
@@ -130,6 +221,15 @@
 
         lax.fori_loop(first, count, step, 0)
 
+    me = block(pos, core)
+    devices = 2 * plane
+    fetches = (
+        pltpu.make_async_copy(rows_hbm, rows_ref, fetch_sem.at[0]),
+        pltpu.make_async_copy(codes_hbm, codes_ref, fetch_sem.at[1]),
+        pltpu.make_async_copy(item_ref, table_ref, fetch_sem.at[2]),
+    )
+    for fetch in fetches:
+        fetch.start()
     barrier = pltpu.get_barrier_semaphore()
     greeted = 1
     pl.semaphore_signal(barrier, inc=1, device_id=partner, device_id_type=pl.DeviceIdType.MESH)
@@ -140,6 +240,8 @@
                 barrier, inc=1, device_id=device(ahead(only(a, k)), core), device_id_type=pl.DeviceIdType.MESH
             )
     pl.semaphore_wait(barrier, greeted)
+    for fetch in fetches:
+        fetch.wait()
 
     def pair_copy(at):
         return remote(part.at[0, at], pair.at[at], pair_send.at[at], pair_recv.at[at], partner)
@@ -294,7 +396,6 @@
 
     lax.fori_loop(0, plane + LAGS[3], reduce_step, 0)
 
-    me = block(pos, core)
     uv = part[1, 0, 0] / hist_len
     pv = part[1, 0, 1]
     gap = jnp.sum(uv * pv, axis=1, keepdims=True) - 1.0
@@ -523,31 +624,8 @@
     groups = 2 * users_dev
     count = users_dev * (hist_len + 1)
     capacity = max(8, (count * 5 // (2 * devices) + 7) // 8 * 8)
-    block = 512
-    padded = round_up(count, block)
-    requests = jnp.concatenate([history_ids.reshape(-1), positive_ids])
-    code = jnp.concatenate(
-        [jnp.arange(users_dev * hist_len, dtype=i32) // hist_len, users_dev + jnp.arange(users_dev, dtype=i32)]
-    )
-    requests = jnp.pad(requests, (0, padded - count), constant_values=devices * rows_dev)
-    code = jnp.pad(code, (0, padded - count))
-    owner = requests // rows_dev
-    local = requests - owner * rows_dev
-
-    lists = pl.pallas_call(
-        functools.partial(route_kernel, devices, capacity, users_dev, block),
-        out_shape=jax.ShapeDtypeStruct((2, devices, capacity), i32),
-        in_specs=[VM] * 3,
-        out_specs=VM,
-        scratch_shapes=[pltpu.VMEM((4 * devices, capacity), f32)],
-        compiler_params=PARAMS,
-        name="route",
-    )(owner[None], local[None], code[None])
-    asked = lax.all_to_all(lists, ("dp", "rows"), split_axis=1, concat_axis=1, tiled=True)
-    rows = asked[0].reshape(-1)
-    codes = asked[1]
     entries = devices * capacity
-    item_gram = jnp.dot(item_table.T, item_table, precision=HIGHEST, preferred_element_type=f32)
+    asks = round_up(hist_len + 1, ROWS_AT_ONCE)
     data, shard = lax.axis_size("dp"), lax.axis_size("rows")
     sizes = line_sizes(data, shard)
     plane = devices // 2
@@ -555,15 +633,40 @@
     unroll = max(n for n in (8, 16, 32, 64, 128) if capacity % n == 0)
     coef = penalty_weight / (rows_dev * devices)
     dma = pltpu.SemaphoreType.DMA
+    list_shape = jax.ShapeDtypeStruct((devices, 1, capacity), i32)
+    rows, codes, item_gram = pl.pallas_call(
+        functools.partial(ask_kernel, data, shard, capacity),
+        out_shape=(list_shape, list_shape, jax.ShapeDtypeStruct((width, width), f32)),
+        in_specs=[VM, VM, HB],
+        out_specs=(HB, HB, VM),
+        scratch_shapes=[
+            pltpu.VMEM((asks, users_dev), i32),
+            pltpu.VMEM((4 * devices, capacity), f32),
+            pltpu.VMEM((devices, 1, capacity), i32),
+            pltpu.VMEM((devices, 1, capacity), i32),
+            pltpu.VMEM((rows_dev, width), f32),
+        ]
+        + [dma((devices,))] * 4
+        + [dma((3,))],
+        compiler_params=pltpu.CompilerParams(
+            vmem_limit_bytes=60 * 1024 * 1024, collective_id=1, has_side_effects=True
+        ),
+        name="ask",
+    )(history_ids.T, positive_ids[None], item_table)
+    flat = rows.reshape(-1)
     vals, user_gram = pl.pallas_call(
         functools.partial(exchange_kernel, sizes, capacity, users_dev, hist_len, coef, unroll),
         out_shape=(
             jax.ShapeDtypeStruct((devices, capacity, width), f32),
             jax.ShapeDtypeStruct((width, width), f32),
         ),
-        in_specs=[SM, SM, VM, VM, VM],
+        in_specs=[HB, HB, VM, VM, HB],
         out_specs=(HB, VM),
         scratch_shapes=[
+            pltpu.SMEM((entries,), i32),
+            pltpu.SMEM((entries,), i32),
+            pltpu.VMEM((rows_dev, width), f32),
+            dma((3,)),
             pltpu.VMEM((capacity, width), f32),
             pltpu.VMEM((2, plane, 2, users_dev, width), f32),
             pltpu.VMEM((plane, 2, users_dev, width), f32),
@@ -591,7 +694,7 @@
             vmem_limit_bytes=60 * 1024 * 1024, collective_id=0, has_side_effects=True
         ),
         name="exchange",
-    )(rows, codes.reshape(-1), codes[:, None, :], item_gram, item_table)
+    )(flat, codes.reshape(-1), codes, item_gram, item_table)
     chunk, tile = min(2048, entries), 256
     return pl.pallas_call(
         functools.partial(scatter_kernel, coef, chunk, 4, tile),
@@ -612,7 +715,7 @@
         + [pltpu.VMEM((rows_dev, width), f32)] * STREAMS,
         compiler_params=PARAMS,
         name="scatter",
-    )(rows, vals.reshape(entries, width), user_gram, item_table, adagrad_state)
+    )(flat, vals.reshape(entries, width), user_gram, item_table, adagrad_state)
 
 
 def solution(mesh):

time: 118 us -> 108 us (0.915)
  Pallas kernels: 95.9 us -> 107 us
  starting transfers between devices: 7.33 us -> 0 us
  matrix products: 6.29 us -> 0 us
  local copies, waits for them, and re-layouts: 5.31 us -> 0 us
  waiting for transfers between devices: 1.51 us -> 0 us
    pallas_call x1, Pallas kernels: 6.13 us -> 19.1 us  [shards(): pl.pallas_call(functools.partial(ask_kernel, data, shard, capacity), out_...]
    all_to_all x1 -> x0, starting transfers between devices: 7.33 us -> none  [shards(): lax.all_to_all(lists, ('dp', 'rows'), split_axis=1, concat_axis=1, tiled=...]
    dot_general x1 -> x0, matrix products: 6.29 us -> none  [shards(): jnp.dot(item_table.T, item_table, precision=HIGHEST, preferred_element_ty...]
    broadcast_in_dim x3 -> x0, local copies, waits for them, and re-layouts: 1.88 us -> none  [the longest x1 0.63 us: shards(): code[None]]
    pallas_call x1, Pallas kernels: 64.2 us -> 62.3 us  [shards(): pl.pallas_call(functools.partial(exchange_kernel, sizes, capacity, users_...]
    pallas_call x1 -> x0, local copies, waits for them, and re-layouts: 1.66 us -> none  [shards(): pl.pallas_call(functools.partial(route_kernel, devices, capacity, users_d...]
    all_to_all x1 -> x0, waiting for transfers between devices: 1.51 us -> none  [shards(): lax.all_to_all(lists, ('dp', 'rows'), split_axis=1, concat_axis=1, tiled=...]
  transfers between devices with their start and end apart: 1 -> 0, of which waited for: 1 -> 0; matrix products, arithmetic and copies ran while one was open for 5% -> 0% of each run, Pallas kernels for 0% -> 0%
where the time goes in v4:
time: 108 us; the launch traced here: 107 us
  Pallas kernels  107 us (99%)
    pallas_call x1, Pallas kernels, shards(): pl.pallas_call(functools.partial(exchange_kernel, sizes, capacity, users_...  62.3 us
    pallas_call x1, Pallas kernels, shards(): pl.pallas_call(functools.partial(scatter_kernel, coef, chunk, 4, tile), o...  25.4 us
    pallas_call x1, Pallas kernels, shards(): pl.pallas_call(functools.partial(ask_kernel, data, shard, capacity), out_...  19.1 us

profile of v4, /device:TPU:0, one launch (start us, length us, event | category | flops | bytes accessed | tf_op | source)
XLA Modules:
  0.0 107.4 jit_solution(6765587577390603057)
XLA Ops:
  0.6 19.1 %ask.1 = (s32[32,1,512]{2,1,0:T(1,128)}, s32[32,1,512]{2,1,0:T(1,128)}, f32[128,128]{1,0:T(8,128)}) custom-call(s32[50,128]{1,0:T(8,128)} %bitcast.9, s32[1,128]{1,0:T(1,128)} %bitcast.10, f32[4096,128]{1,0:T(8,128)} %table_ref.1), custom_call_target="tpu_custom_call" | custom-call | tf_op jit(solution)/shard_map/ask/pallas_call | solution.py:637
  19.8 62.3 %exchange.1 = (f32[32,512,128]{2,1,0:T(8,128)}, f32[128,128]{1,0:T(8,128)}) custom-call(s32[16384]{0:T(1024)} %bitcast.6, s32[16384]{0:T(1024)} %bitcast.8, s32[32,1,512]{2,1,0:T(1,128)} %get-tuple-element.8.hot_ref, f32[128,128]{1,0:T(8,128)} %get-tuple-element.9.gram_ref, f32[4096,128]{1,0:T(8,128)} %table_ref.1), custom_call_target="tpu_custom_call" | custom-call | tf_op jit(solution)/shard_map/exchange/pallas_call | solution.py:657
  82.1 25.4 %scatter.1 = (f32[4096,128]{1,0:T(8,128)}, f32[4096,128]{1,0:T(8,128)}) custom-call(s32[16384]{0:T(1024)} %bitcast.7, f32[16384,128]{1,0:T(8,128)} %bitcast.5, f32[128,128]{1,0:T(8,128)} %get-tuple-element.11.ugram_ref, f32[4096,128]{1,0:T(8,128)} %table_ref.1, f32[4096,128]{1,0:T(8,128)} %state_ref.1), custom_call_target="tpu_custom_call" | custom-call | tf_op jit(solution)/shard_map/scatter/pallas_call | solution.py:699

commit v5 on v4

--- a/solution.py
+++ b/solution.py
@@ -10,7 +10,7 @@
 penalty_weight = 10.0
 step_size = 0.05
 LOW = 128
-STREAMS = 8
+STREAMS = 16
 HIGHEST = lax.Precision.HIGHEST
 f32, bf16, i32 = jnp.float32, jnp.bfloat16, jnp.int32
 
@@ -523,8 +523,8 @@
 
 def scatter_kernel(
     coef, chunk, unroll, tile,
-    rows_ref, vals_ref, ugram_ref, table_ref, state_ref, new_table_ref, new_state_ref,
-    vbuf, table, state, vsem, in_sem, out_sem, *accs,
+    rows_hbm, vals_ref, ugram_ref, table_ref, state_ref, new_table_ref, new_state_ref,
+    rows_ref, vbuf, table, state, vsem, in_sem, out_sem, *accs,
 ):
     entries = rows_ref.shape[0]
     chunks = entries // chunk
@@ -540,6 +540,8 @@
 
     table_copy = pltpu.make_async_copy(table_ref, table, in_sem.at[0])
     state_copy = pltpu.make_async_copy(state_ref, state, in_sem.at[1])
+    rows_copy = pltpu.make_async_copy(rows_hbm, rows_ref, in_sem.at[2])
+    rows_copy.start()
     vals_copy(0).start()
     vals_copy(1).start()
     table_copy.start()
@@ -573,6 +575,7 @@
 
         return 0
 
+    rows_copy.wait()
     lax.fori_loop(0, chunks, one, 0)
     table_copy.wait()
     state_copy.wait()
@@ -596,7 +599,7 @@
         g = g + add
         new = state[at, :] + g * g
         state[at, :] = new
-        table[at, :] = item - step_size * g / jnp.sqrt(new)
+        table[at, :] = item - step_size * g * lax.rsqrt(new)
         out_copy(t, 0).start()
         out_copy(t, 1).start()
         return 0
@@ -695,21 +698,22 @@
         ),
         name="exchange",
     )(flat, codes.reshape(-1), codes, item_gram, item_table)
-    chunk, tile = min(2048, entries), 256
+    chunk, tile = min(4096, entries), 512
     return pl.pallas_call(
-        functools.partial(scatter_kernel, coef, chunk, 4, tile),
+        functools.partial(scatter_kernel, coef, chunk, 8, tile),
         out_shape=(
             jax.ShapeDtypeStruct(item_table.shape, f32),
             jax.ShapeDtypeStruct(item_table.shape, f32),
         ),
-        in_specs=[SM, HB, VM, HB, HB],
+        in_specs=[HB, HB, VM, HB, HB],
         out_specs=(HB, HB),
         scratch_shapes=[
+            pltpu.SMEM((entries,), i32),
             pltpu.VMEM((2, chunk, width), f32),
             pltpu.VMEM((rows_dev, width), f32),
             pltpu.VMEM((rows_dev, width), f32),
             dma((2,)),
-            dma((2,)),
+            dma((3,)),
             dma((2, rows_dev // tile)),
         ]
         + [pltpu.VMEM((rows_dev, width), f32)] * STREAMS,

time: 108 us -> 102 us (0.944)
  Pallas kernels: 107 us -> 101 us
    pallas_call x1, Pallas kernels: 25.4 us -> 19.1 us  [shards(): pl.pallas_call(functools.partial(scatter_kernel, coef, chunk, 8, tile), o...]
where the time goes in v5:
time: 102 us; the launch traced here: 101 us
  Pallas kernels  101 us (99%)
    pallas_call x1, Pallas kernels, shards(): pl.pallas_call(functools.partial(exchange_kernel, sizes, capacity, users_...  62.3 us
    pallas_call x1, Pallas kernels, shards(): pl.pallas_call(functools.partial(ask_kernel, data, shard, capacity), out_...  19.1 us
    pallas_call x1, Pallas kernels, shards(): pl.pallas_call(functools.partial(scatter_kernel, coef, chunk, 8, tile), o...  19.1 us

profile of v5, /device:TPU:0, one launch (start us, length us, event | category | flops | bytes accessed | tf_op | source)
XLA Modules:
  0.0 101.2 jit_solution(12420564099639992272)
XLA Ops:
  0.6 19.1 %ask.1 = (s32[32,1,512]{2,1,0:T(1,128)}, s32[32,1,512]{2,1,0:T(1,128)}, f32[128,128]{1,0:T(8,128)}) custom-call(s32[50,128]{1,0:T(8,128)} %bitcast.9, s32[1,128]{1,0:T(1,128)} %bitcast.10, f32[4096,128]{1,0:T(8,128)} %table_ref.1), custom_call_target="tpu_custom_call" | custom-call | tf_op jit(solution)/shard_map/ask/pallas_call | solution.py:640
  19.8 62.3 %exchange.1 = (f32[32,512,128]{2,1,0:T(8,128)}, f32[128,128]{1,0:T(8,128)}) custom-call(s32[16384]{0:T(1024)} %bitcast.6, s32[16384]{0:T(1024)} %bitcast.8, s32[32,1,512]{2,1,0:T(1,128)} %get-tuple-element.8.hot_ref, f32[128,128]{1,0:T(8,128)} %get-tuple-element.9.gram_ref, f32[4096,128]{1,0:T(8,128)} %table_ref.1), custom_call_target="tpu_custom_call" | custom-call | tf_op jit(solution)/shard_map/exchange/pallas_call | solution.py:660
  82.1 19.1 %scatter.1 = (f32[4096,128]{1,0:T(8,128)}, f32[4096,128]{1,0:T(8,128)}) custom-call(s32[16384]{0:T(1024)} %bitcast.7, f32[16384,128]{1,0:T(8,128)} %bitcast.5, f32[128,128]{1,0:T(8,128)} %get-tuple-element.11.ugram_ref, f32[4096,128]{1,0:T(8,128)} %table_ref.1, f32[4096,128]{1,0:T(8,128)} %state_ref.1), custom_call_target="tpu_custom_call" | custom-call | tf_op jit(solution)/shard_map/scatter/pallas_call | solution.py:702

commit v6 on v5

--- a/solution.py
+++ b/solution.py
@@ -89,7 +89,9 @@
         acc[...] += lax.dot_general(left, right, (((1,), (1,)), ((), ())), preferred_element_type=f32)
         return carry + jnp.sum(member, axis=1, keepdims=True)
 
-    lax.fori_loop(0, asks // ROWS_AT_ONCE, route, jnp.zeros((devices, 1), f32))
+    carry = jnp.zeros((devices, 1), f32)
+    for j in range(asks // ROWS_AT_ONCE):
+        carry = route(j, carry)
 
     def write(d):
         row = acc[pl.ds(d, 1), :] * LOW + acc[pl.ds(devices + d, 1), :]
@@ -98,7 +100,8 @@
         rows[d] = row.astype(i32)
         codes[d] = jnp.where(present > 0.5, code, 2.0 * users_dev).astype(i32)
 
-    each(0, devices, write)
+    for d in range(devices):
+        write(d)
     pl.semaphore_wait(barrier, devices - 1)
 
     def list_copies(k, to, at):
@@ -156,7 +159,7 @@
 ORDERS = ((0, 1, 2), (1, 0, 2))
 LAGS = (2, 4, 6, 8)
 VSLOTS = 4
-ROWS_AT_ONCE = 4
+ROWS_AT_ONCE = 8
 TWIN_LAG = 2
 
 

time: 102 us -> 98.8 us (0.969)
  Pallas kernels: 101 us -> 97.8 us
    pallas_call x1, Pallas kernels: 19.1 us -> 16.4 us  [shards(): pl.pallas_call(functools.partial(ask_kernel, data, shard, capacity), out_...]
where the time goes in v6:
time: 98.8 us; the launch traced here: 98.5 us
  Pallas kernels  97.8 us (99%)
    pallas_call x1, Pallas kernels, shards(): pl.pallas_call(functools.partial(exchange_kernel, sizes, capacity, users_...  62.3 us
    pallas_call x1, Pallas kernels, shards(): pl.pallas_call(functools.partial(scatter_kernel, coef, chunk, 8, tile), o...  19.1 us
    pallas_call x1, Pallas kernels, shards(): pl.pallas_call(functools.partial(ask_kernel, data, shard, capacity), out_...  16.4 us

profile of v6, /device:TPU:0, one launch (start us, length us, event | category | flops | bytes accessed | tf_op | source)
XLA Modules:
  0.0 98.5 jit_solution(13260189090857055276)
XLA Ops:
  0.6 16.4 %ask.1 = (s32[32,1,512]{2,1,0:T(1,128)}, s32[32,1,512]{2,1,0:T(1,128)}, f32[128,128]{1,0:T(8,128)}) custom-call(s32[50,128]{1,0:T(8,128)} %bitcast.9, s32[1,128]{1,0:T(1,128)} %bitcast.10, f32[4096,128]{1,0:T(8,128)} %table_ref.1), custom_call_target="tpu_custom_call" | custom-call | tf_op jit(solution)/shard_map/ask/pallas_call | solution.py:643
  17.1 62.3 %exchange.1 = (f32[32,512,128]{2,1,0:T(8,128)}, f32[128,128]{1,0:T(8,128)}) custom-call(s32[16384]{0:T(1024)} %bitcast.6, s32[16384]{0:T(1024)} %bitcast.8, s32[32,1,512]{2,1,0:T(1,128)} %get-tuple-element.8.hot_ref, f32[128,128]{1,0:T(8,128)} %get-tuple-element.9.gram_ref, f32[4096,128]{1,0:T(8,128)} %table_ref.1), custom_call_target="tpu_custom_call" | custom-call | tf_op jit(solution)/shard_map/exchange/pallas_call | solution.py:663
  79.4 19.1 %scatter.1 = (f32[4096,128]{1,0:T(8,128)}, f32[4096,128]{1,0:T(8,128)}) custom-call(s32[16384]{0:T(1024)} %bitcast.7, f32[16384,128]{1,0:T(8,128)} %bitcast.5, f32[128,128]{1,0:T(8,128)} %get-tuple-element.11.ugram_ref, f32[4096,128]{1,0:T(8,128)} %table_ref.1, f32[4096,128]{1,0:T(8,128)} %state_ref.1), custom_call_target="tpu_custom_call" | custom-call | tf_op jit(solution)/shard_map/scatter/pallas_call | solution.py:705

commit v7 on v6

--- a/solution.py
+++ b/solution.py
@@ -25,8 +25,8 @@
 
 
 def ask_kernel(
-    data, shard, capacity, hist_ref, pos_ref, item_ref, rows_ref, codes_ref, gram_ref,
-    ids, acc, rows, codes, table_ref, row_send, row_recv, code_send, code_recv, own_sem,
+    data, shard, capacity, hist_ref, pos_ref, item_ref, rows_ref, codes_ref, gram_hbm,
+    gram_ref, ids, acc, rows, codes, table_ref, row_send, row_recv, code_send, code_recv, own_sem,
 ):
     devices = data * shard
     hist_len, users_dev = hist_ref.shape
@@ -139,6 +139,8 @@
         gram_ref[...] += both[:, :width] + (both[:, width:] + both[:, width:].T)
 
     each(0, rows_dev // tall, square)
+    gram_copy = pltpu.make_async_copy(gram_ref, gram_hbm, own_sem.at[3])
+    gram_copy.start()
 
     def finish(k):
         n = lax.rem(me - k + devices, devices)
@@ -149,6 +151,7 @@
     each(1, devices, finish)
     for copy in own:
         copy.wait()
+    gram_copy.wait()
 
 
 def line_sizes(data, shard):
@@ -165,8 +168,8 @@
 
 def exchange_kernel(
     sizes, capacity, users_dev, hist_len, coef, unroll,
-    rows_hbm, codes_hbm, hot_ref, gram_ref, item_ref, vals_ref, ugram_ref,
-    rows_ref, codes_ref, table_ref, fetch_sem, picked, part, pair, mail, grads, cur, vbuf, upart, gsum, gmail, gfull,
+    rows_hbm, codes_hbm, hot_hbm, gram_hbm, item_ref, vals_ref, ugram_hbm,
+    rows_ref, codes_ref, hot_ref, gram_ref, table_ref, fetch_sem, picked, part, pair, mail, grads, cur, vbuf, upart, gsum, gmail, gfull,
     pair_send, pair_recv, mail_send, mail_recv, ag_send, ag_recv, twin_send, twin_recv, gram_send, gram_recv, vsem,
 ):
     nx, ny, nz = sizes
@@ -206,7 +209,7 @@
         out = [0, 0, 0]
         for a in reversed(digits):
             out[a] = lax.rem(n, sizes[a])
-            n = n // sizes[a]
+            n = lax.div(n, sizes[a])
         return tuple(out)
 
     partner = device(pos, 1 - core)
@@ -230,6 +233,8 @@
         pltpu.make_async_copy(rows_hbm, rows_ref, fetch_sem.at[0]),
         pltpu.make_async_copy(codes_hbm, codes_ref, fetch_sem.at[1]),
         pltpu.make_async_copy(item_ref, table_ref, fetch_sem.at[2]),
+        pltpu.make_async_copy(hot_hbm, hot_ref, fetch_sem.at[3]),
+        pltpu.make_async_copy(gram_hbm, gram_ref, fetch_sem.at[4]),
     )
     for fetch in fetches:
         fetch.start()
@@ -505,7 +510,8 @@
         return 0
 
     lax.fori_loop(0, plane + vals_delay + TWIN_LAG, spread, 0)
-    ugram_ref[...] = gfull[1]
+    ugram_copy = pltpu.make_async_copy(gfull.at[1], ugram_hbm, fetch_sem.at[5])
+    ugram_copy.start()
 
     def drain(n):
         pair_copy(n).wait_send()
@@ -522,12 +528,13 @@
     gram_drain(0, gram_ref)
     gram_drain(1, upart)
     each(0, VSLOTS, lambda v: vals_copy(v, me).wait())
+    ugram_copy.wait()
 
 
 def scatter_kernel(
     coef, chunk, unroll, tile,
-    rows_hbm, vals_ref, ugram_ref, table_ref, state_ref, new_table_ref, new_state_ref,
-    rows_ref, vbuf, table, state, vsem, in_sem, out_sem, *accs,
+    rows_hbm, vals_ref, ugram_hbm, table_ref, state_ref, new_table_ref, new_state_ref,
+    rows_ref, ugram_ref, vbuf, table, state, vsem, in_sem, out_sem, *accs,
 ):
     entries = rows_ref.shape[0]
     chunks = entries // chunk
@@ -544,11 +551,13 @@
     table_copy = pltpu.make_async_copy(table_ref, table, in_sem.at[0])
     state_copy = pltpu.make_async_copy(state_ref, state, in_sem.at[1])
     rows_copy = pltpu.make_async_copy(rows_hbm, rows_ref, in_sem.at[2])
+    ugram_copy = pltpu.make_async_copy(ugram_hbm, ugram_ref, in_sem.at[3])
     rows_copy.start()
     vals_copy(0).start()
     vals_copy(1).start()
     table_copy.start()
     state_copy.start()
+    ugram_copy.start()
     for acc in accs:
         acc[...] = jnp.zeros_like(acc)
 
@@ -582,6 +591,7 @@
     lax.fori_loop(0, chunks, one, 0)
     table_copy.wait()
     state_copy.wait()
+    ugram_copy.wait()
     u0, u1 = split2(ugram_ref[...])
     u00 = jnp.concatenate([u0, u0], axis=0)
 
@@ -644,8 +654,9 @@
         functools.partial(ask_kernel, data, shard, capacity),
         out_shape=(list_shape, list_shape, jax.ShapeDtypeStruct((width, width), f32)),
         in_specs=[VM, VM, HB],
-        out_specs=(HB, HB, VM),
+        out_specs=(HB, HB, HB),
         scratch_shapes=[
+            pltpu.VMEM((width, width), f32),
             pltpu.VMEM((asks, users_dev), i32),
             pltpu.VMEM((4 * devices, capacity), f32),
             pltpu.VMEM((devices, 1, capacity), i32),
@@ -653,7 +664,7 @@
             pltpu.VMEM((rows_dev, width), f32),
         ]
         + [dma((devices,))] * 4
-        + [dma((3,))],
+        + [dma((4,))],
         compiler_params=pltpu.CompilerParams(
             vmem_limit_bytes=60 * 1024 * 1024, collective_id=1, has_side_effects=True
         ),
@@ -666,13 +677,15 @@
             jax.ShapeDtypeStruct((devices, capacity, width), f32),
             jax.ShapeDtypeStruct((width, width), f32),
         ),
-        in_specs=[HB, HB, VM, VM, HB],
-        out_specs=(HB, VM),
+        in_specs=[HB, HB, HB, HB, HB],
+        out_specs=(HB, HB),
         scratch_shapes=[
             pltpu.SMEM((entries,), i32),
             pltpu.SMEM((entries,), i32),
+            pltpu.VMEM((devices, 1, capacity), i32),
+            pltpu.VMEM((width, width), f32),
             pltpu.VMEM((rows_dev, width), f32),
-            dma((3,)),
+            dma((6,)),
             pltpu.VMEM((capacity, width), f32),
             pltpu.VMEM((2, plane, 2, users_dev, width), f32),
             pltpu.VMEM((plane, 2, users_dev, width), f32),
@@ -708,15 +721,16 @@
             jax.ShapeDtypeStruct(item_table.shape, f32),
             jax.ShapeDtypeStruct(item_table.shape, f32),
         ),
-        in_specs=[HB, HB, VM, HB, HB],
+        in_specs=[HB, HB, HB, HB, HB],
         out_specs=(HB, HB),
         scratch_shapes=[
             pltpu.SMEM((entries,), i32),
+            pltpu.VMEM((width, width), f32),
             pltpu.VMEM((2, chunk, width), f32),
             pltpu.VMEM((rows_dev, width), f32),
             pltpu.VMEM((rows_dev, width), f32),
             dma((2,)),
-            dma((3,)),
+            dma((4,)),
             dma((2, rows_dev // tile)),
         ]
         + [pltpu.VMEM((rows_dev, width), f32)] * STREAMS,

time: 98.8 us -> 96.2 us (0.974); the launches traced: 98.5 us -> 94.8 us
  Pallas kernels: 97.8 us -> 94.2 us
    pallas_call x1, Pallas kernels: 62.3 us -> 60.6 us  [shards(): pl.pallas_call(functools.partial(exchange_kernel, sizes, capacity, users_...]
    pallas_call x1, Pallas kernels: 19.1 us -> 17.8 us  [shards(): pl.pallas_call(functools.partial(scatter_kernel, coef, chunk, 8, tile), o...]
where the time goes in v7:
time: 96.2 us; the launch traced here: 94.8 us
  Pallas kernels  94.2 us (98%)
    pallas_call x1, Pallas kernels, shards(): pl.pallas_call(functools.partial(exchange_kernel, sizes, capacity, users_...  60.6 us
    pallas_call x1, Pallas kernels, shards(): pl.pallas_call(functools.partial(scatter_kernel, coef, chunk, 8, tile), o...  17.8 us
    pallas_call x1, Pallas kernels, shards(): pl.pallas_call(functools.partial(ask_kernel, data, shard, capacity), out_...  15.8 us

profile of v7, /device:TPU:0, one launch (start us, length us, event | category | flops | bytes accessed | tf_op | source)
XLA Modules:
  0.0 94.8 jit_solution(17198565069631019639)
XLA Ops:
  0.6 15.8 %ask.1 = (s32[32,1,512]{2,1,0:T(1,128)}, s32[32,1,512]{2,1,0:T(1,128)}, f32[128,128]{1,0:T(8,128)}) custom-call(s32[50,128]{1,0:T(8,128)} %bitcast.9, s32[1,128]{1,0:T(1,128)} %bitcast.10, f32[4096,128]{1,0:T(8,128)} %table_ref.1), custom_call_target="tpu_custom_call" | custom-call | tf_op jit(solution)/shard_map/ask/pallas_call | solution.py:653
  16.5 60.6 %exchange.1 = (f32[32,512,128]{2,1,0:T(8,128)}, f32[128,128]{1,0:T(8,128)}) custom-call(s32[16384]{0:T(1024)} %bitcast.6, s32[16384]{0:T(1024)} %bitcast.8, s32[32,1,512]{2,1,0:T(1,128)} %get-tuple-element.8.hot_hbm, f32[128,128]{1,0:T(8,128)} %get-tuple-element.9.gram_hbm, f32[4096,128]{1,0:T(8,128)} %table_ref.1), custom_call_target="tpu_custom_call" | custom-call | tf_op jit(solution)/shard_map/exchange/pallas_call | solution.py:674
  77.1 17.8 %scatter.1 = (f32[4096,128]{1,0:T(8,128)}, f32[4096,128]{1,0:T(8,128)}) custom-call(s32[16384]{0:T(1024)} %bitcast.7, f32[16384,128]{1,0:T(8,128)} %bitcast.5, f32[128,128]{1,0:T(8,128)} %get-tuple-element.11.ugram_hbm, f32[4096,128]{1,0:T(8,128)} %table_ref.1, f32[4096,128]{1,0:T(8,128)} %state_ref.1), custom_call_target="tpu_custom_call" | custom-call | tf_op jit(solution)/shard_map/scatter/pallas_call | solution.py:718

commit v8 on v7

--- a/solution.py
+++ b/solution.py
@@ -25,11 +25,11 @@
 
 
 def ask_kernel(
-    data, shard, capacity, hist_ref, pos_ref, item_ref, rows_ref, codes_ref, gram_hbm,
+    data, shard, capacity, hist_hbm, pos_hbm, item_ref, rows_ref, codes_ref, gram_hbm,
     gram_ref, ids, acc, rows, codes, table_ref, row_send, row_recv, code_send, code_recv, own_sem,
 ):
     devices = data * shard
-    hist_len, users_dev = hist_ref.shape
+    hist_len, users_dev = hist_hbm.shape
     width = item_ref.shape[1]
     dp, rw = lax.axis_index("dp"), lax.axis_index("rows")
 
@@ -43,6 +43,12 @@
     me = dp * shard + rw
     rows_dev = item_ref.shape[0]
     item_copy = pltpu.make_async_copy(item_ref, table_ref, own_sem.at[2])
+    ids_copies = (
+        pltpu.make_async_copy(hist_hbm, ids.at[pl.ds(0, hist_len)], own_sem.at[4]),
+        pltpu.make_async_copy(pos_hbm, ids.at[pl.ds(hist_len, 1)], own_sem.at[5]),
+    )
+    for copy in ids_copies:
+        copy.start()
     item_copy.start()
     barrier = pltpu.get_barrier_semaphore()
 
@@ -56,8 +62,6 @@
 
     each(1, devices, greet)
     asks = ids.shape[0]
-    ids[0:hist_len, :] = hist_ref[...]
-    ids[hist_len : hist_len + 1, :] = pos_ref[...]
     if asks > hist_len + 1:
         ids[hist_len + 1 :, :] = jnp.full((asks - hist_len - 1, users_dev), devices * rows_dev, i32)
     wide = ROWS_AT_ONCE * users_dev
@@ -89,6 +93,8 @@
         acc[...] += lax.dot_general(left, right, (((1,), (1,)), ((), ())), preferred_element_type=f32)
         return carry + jnp.sum(member, axis=1, keepdims=True)
 
+    for copy in ids_copies:
+        copy.wait()
     carry = jnp.zeros((devices, 1), f32)
     for j in range(asks // ROWS_AT_ONCE):
         carry = route(j, carry)
@@ -162,6 +168,7 @@
 ORDERS = ((0, 1, 2), (1, 0, 2))
 LAGS = (2, 4, 6, 8)
 VSLOTS = 4
+GRAM_ORDERS = ((2, 0, 1), (0, 1, 2))
 ROWS_AT_ONCE = 8
 TWIN_LAG = 2
 
@@ -273,10 +280,11 @@
     def gram_pair(t, src):
         return remote(src.at[theirs], gmail.at[t, 0], gram_send.at[t, 0], gram_recv.at[t, 0], partner)
 
-    def gram_line(t, a, k):
+    def gram_line(t, s, k):
+        a = GRAM_ORDERS[t][s]
         at = first[a] + k - 1
         return remote(
-            gsum.at[t, a], gmail.at[t, at], gram_send.at[t, at], gram_recv.at[t, at], device(ahead(only(a, k)), core)
+            gsum.at[t, s], gmail.at[t, at], gram_send.at[t, at], gram_recv.at[t, at], device(ahead(only(a, k)), core)
         )
 
     def gram_final(t):
@@ -285,21 +293,22 @@
     def gram_open(t, src):
         gram_pair(t, src).start()
 
-    def gram_send_line(t, a):
-        for k in range(1, sizes[a]):
-            gram_line(t, a, k).start()
+    def gram_send_line(t, s):
+        for k in range(1, sizes[GRAM_ORDERS[t][s]]):
+            gram_line(t, s, k).start()
 
     def gram_step(t, src, stage):
         if stage == 0:
             gram_pair(t, src).wait_recv()
             gsum[t, 0] = src[mine, :] + gmail[t, 0]
         elif stage <= 3:
-            a = stage - 1
-            total = gsum[t, a]
+            s = stage - 1
+            a = GRAM_ORDERS[t][s]
+            total = gsum[t, s]
             for k in range(1, sizes[a]):
-                gram_line(t, a, k).wait_recv()
+                gram_line(t, s, k).wait_recv()
                 total = total + gmail[t, first[a] + k - 1]
-            gsum[t, a + 1] = total
+            gsum[t, s + 1] = total
         else:
             gram_final(t).wait_recv()
         if stage < 3:
@@ -310,9 +319,9 @@
 
     def gram_drain(t, src):
         gram_pair(t, src).wait_send()
-        for a in axes:
-            for k in range(1, sizes[a]):
-                gram_line(t, a, k).wait_send()
+        for s in range(3):
+            for k in range(1, sizes[GRAM_ORDERS[t][s]]):
+                gram_line(t, s, k).wait_send()
         gram_final(t).wait_send()
 
     codes_to = lax.broadcasted_iota(i32, (2 * users_dev, capacity), 0)
@@ -378,7 +387,7 @@
                                 leave(h, r, order[stage])
 
         for stage in range(5):
-            @pl.when(i == 3 * stage + 3)
+            @pl.when(i == 3 * stage + 1)
             def _():
                 gram_step(0, gram_ref, stage)
 
@@ -653,7 +662,7 @@
     rows, codes, item_gram = pl.pallas_call(
         functools.partial(ask_kernel, data, shard, capacity),
         out_shape=(list_shape, list_shape, jax.ShapeDtypeStruct((width, width), f32)),
-        in_specs=[VM, VM, HB],
+        in_specs=[HB, HB, HB],
         out_specs=(HB, HB, HB),
         scratch_shapes=[
             pltpu.VMEM((width, width), f32),
@@ -664,7 +673,7 @@
             pltpu.VMEM((rows_dev, width), f32),
         ]
         + [dma((devices,))] * 4
-        + [dma((4,))],
+        + [dma((6,))],
         compiler_params=pltpu.CompilerParams(
             vmem_limit_bytes=60 * 1024 * 1024, collective_id=1, has_side_effects=True
         ),

time: 96.2 us -> 94.9 us (0.986)
    pallas_call x1, Pallas kernels: 60.6 us -> 59.6 us  [shards(): pl.pallas_call(functools.partial(exchange_kernel, sizes, capacity, users_...]
where the time goes in v8:
time: 94.9 us; the launch traced here: 94.3 us
  Pallas kernels  93.7 us (99%)
    pallas_call x1, Pallas kernels, shards(): pl.pallas_call(functools.partial(exchange_kernel, sizes, capacity, users_...  59.6 us
    pallas_call x1, Pallas kernels, shards(): pl.pallas_call(functools.partial(scatter_kernel, coef, chunk, 8, tile), o...  18.6 us
    pallas_call x1, Pallas kernels, shards(): pl.pallas_call(functools.partial(ask_kernel, data, shard, capacity), out_...  15.5 us

profile of v8, /device:TPU:0, one launch (start us, length us, event | category | flops | bytes accessed | tf_op | source)
XLA Modules:
  0.0 94.3 jit_solution(6651518212886643031)
XLA Ops:
  0.6 15.5 %ask.1 = (s32[32,1,512]{2,1,0:T(1,128)}, s32[32,1,512]{2,1,0:T(1,128)}, f32[128,128]{1,0:T(8,128)}) custom-call(s32[50,128]{1,0:T(8,128)} %bitcast.9, s32[1,128]{1,0:T(1,128)} %bitcast.10, f32[4096,128]{1,0:T(8,128)} %table_ref.1), custom_call_target="tpu_custom_call" | custom-call | tf_op jit(solution)/shard_map/ask/pallas_call | solution.py:662
  16.1 59.6 %exchange.1 = (f32[32,512,128]{2,1,0:T(8,128)}, f32[128,128]{1,0:T(8,128)}) custom-call(s32[16384]{0:T(1024)} %bitcast.6, s32[16384]{0:T(1024)} %bitcast.8, s32[32,1,512]{2,1,0:T(1,128)} %get-tuple-element.8.hot_hbm, f32[128,128]{1,0:T(8,128)} %get-tuple-element.9.gram_hbm, f32[4096,128]{1,0:T(8,128)} %table_ref.1), custom_call_target="tpu_custom_call" | custom-call | tf_op jit(solution)/shard_map/exchange/pallas_call | solution.py:683
  75.7 18.6 %scatter.1 = (f32[4096,128]{1,0:T(8,128)}, f32[4096,128]{1,0:T(8,128)}) custom-call(s32[16384]{0:T(1024)} %bitcast.7, f32[16384,128]{1,0:T(8,128)} %bitcast.5, f32[128,128]{1,0:T(8,128)} %get-tuple-element.11.ugram_hbm, f32[4096,128]{1,0:T(8,128)} %table_ref.1, f32[4096,128]{1,0:T(8,128)} %state_ref.1), custom_call_target="tpu_custom_call" | custom-call | tf_op jit(solution)/shard_map/scatter/pallas_call | solution.py:727

commit v9 on v8

--- a/solution.py
+++ b/solution.py
@@ -723,9 +723,9 @@
         ),
         name="exchange",
     )(flat, codes.reshape(-1), codes, item_gram, item_table)
-    chunk, tile = min(4096, entries), 512
+    chunk, tile = min(4096, entries), 1024
     return pl.pallas_call(
-        functools.partial(scatter_kernel, coef, chunk, 8, tile),
+        functools.partial(scatter_kernel, coef, chunk, 16, tile),
         out_shape=(
             jax.ShapeDtypeStruct(item_table.shape, f32),
             jax.ShapeDtypeStruct(item_table.shape, f32),

time: 94.9 us -> 93.7 us (0.987)
  no operation moved by 1% of the time
where the time goes in v9:
time: 93.7 us; the launch traced here: 93.8 us
  Pallas kernels  93.1 us (99%)
    pallas_call x1, Pallas kernels, shards(): pl.pallas_call(functools.partial(exchange_kernel, sizes, capacity, users_...  59.6 us
    pallas_call x1, Pallas kernels, shards(): pl.pallas_call(functools.partial(scatter_kernel, coef, chunk, 16, tile),...  18 us
    pallas_call x1, Pallas kernels, shards(): pl.pallas_call(functools.partial(ask_kernel, data, shard, capacity), out_...  15.5 us

profile of v9, /device:TPU:0, one launch (start us, length us, event | category | flops | bytes accessed | tf_op | source)
XLA Modules:
  0.0 93.8 jit_solution(5921699859759575068)
XLA Ops:
  0.6 15.5 %ask.1 = (s32[32,1,512]{2,1,0:T(1,128)}, s32[32,1,512]{2,1,0:T(1,128)}, f32[128,128]{1,0:T(8,128)}) custom-call(s32[50,128]{1,0:T(8,128)} %bitcast.9, s32[1,128]{1,0:T(1,128)} %bitcast.10, f32[4096,128]{1,0:T(8,128)} %table_ref.1), custom_call_target="tpu_custom_call" | custom-call | tf_op jit(solution)/shard_map/ask/pallas_call | solution.py:662
  16.1 59.6 %exchange.1 = (f32[32,512,128]{2,1,0:T(8,128)}, f32[128,128]{1,0:T(8,128)}) custom-call(s32[16384]{0:T(1024)} %bitcast.6, s32[16384]{0:T(1024)} %bitcast.8, s32[32,1,512]{2,1,0:T(1,128)} %get-tuple-element.8.hot_hbm, f32[128,128]{1,0:T(8,128)} %get-tuple-element.9.gram_hbm, f32[4096,128]{1,0:T(8,128)} %table_ref.1), custom_call_target="tpu_custom_call" | custom-call | tf_op jit(solution)/shard_map/exchange/pallas_call | solution.py:683
  75.8 18.0 %scatter.1 = (f32[4096,128]{1,0:T(8,128)}, f32[4096,128]{1,0:T(8,128)}) custom-call(s32[16384]{0:T(1024)} %bitcast.7, f32[16384,128]{1,0:T(8,128)} %bitcast.5, f32[128,128]{1,0:T(8,128)} %get-tuple-element.11.ugram_hbm, f32[4096,128]{1,0:T(8,128)} %table_ref.1, f32[4096,128]{1,0:T(8,128)} %state_ref.1), custom_call_target="tpu_custom_call" | custom-call | tf_op jit(solution)/shard_map/scatter/pallas_call | solution.py:727
